TPU v7x, 32 devices: a whole 2x2x4 slice. The times are simulated.
32 devices in a mesh: space: 16 (over z, y, x), level: 2 (over core).
Axes of the slice: x: 2, y: 2, z: 4, core: 2. Of those that a mesh axis runs over, the one named last changes fastest.
Arguments:
- velocity: float32 [2, 16, 16384], P(None, 'level', 'space'), may hold values from -3 to 3
- density: float32 [16, 16384], P('level', 'space'), may hold values from -6 to 6
- elevation: float32 [16384], P('space'), may hold values from -3 to 3
- grad_weights: float32 [2, 6, 16384], P(None, None, 'space'), may hold values from -2.4 to 2.4
- lap_weights: float32 [6, 16384], P(None, 'space'), may hold values from 0.02 to 0.2
- coriolis: float32 [16384], P('space'), may hold values from 0.5 to 2
- node_area: float32 [16384], P('space'), may hold values from 1 to 100, as said below
- thickness: float32 [16], P('level'), may hold values from 0.5 to 2
- send_list: int32 [16, 256], P('space'), may hold values from 0 to 1023
- neighbours: int32 [6, 16384], P(None, 'space'), may hold values from 0 to 1279
- bottom: int32 [16384], P('space'), may hold values from 0 to 16, as said below
Outputs:
- velocity_out: float32 [2, 16, 16384], P(None, 'level', 'space')
- density_out: float32 [16, 16384], P('level', 'space')
- elevation_out: float32 [16384], P('space')
- volume_drift: float32 [4], replicated
Inputs may be any that keep to these rules, and one draw needn't show every extreme that they name: `send_list`: local node numbers within the sending partition; the first 128 go to the partition one below along space, the other 128 to the one above. `neighbours`: slots below 1024 are the partition's own nodes; the next 128 are halo slots filled from the partition below, the last 128 from the partition above. Levels of a node are wet from the surface down to bottom - 1; a node with 0 is dry. Some partitions are shallower than others. `node_area`: positive areas.
All inputs are finite; a program needn't handle non-finite values.
Results may differ from a plain program's by a relative error of at most 0.00013.
Values sent between devices are 32-bit elements; how exact they have to be, the bound alone decides.
No kernel may reach another device: no remote copies, remote signals or barrier semaphores. Data moves between devices by JAX's collectives and lax.ppermute only.
A program may use at most 64 MiB of HBM per device.

v0:
```python
import jax
import jax.numpy as jnp
from jax import lax
from jax.sharding import PartitionSpec as P

STEPS = 4


time_step = 0.1
buoyancy = 0.5
drag_rate = 0.5


def extended_2(array, sides, width):
    for axis, dim in sides:
        devices, length = (lax.axis_size(axis), array.shape[dim])
        up = [(i, (i + 1) % devices) for i in range(devices - 1)]
        down = [(j, i) for i, j in up]
        last = lax.slice_in_dim(array, length - width, length, axis=dim)
        first = lax.slice_in_dim(array, 0, width, axis=dim)
        before = lax.ppermute(last, axis, up)
        after = lax.ppermute(first, axis, down)
        array = jnp.concatenate([before, array, after], axis=dim)
    return array


def prefix(value, axis, join, neutral):
    count, mine = (lax.axis_size(axis), lax.axis_index(axis))
    pieces = lax.all_gather(value, axis)
    total = jnp.full_like(value, 0) + jnp.asarray(neutral, value.dtype)

    def hop(position, total):
        longer = join(total, pieces[position])
        return jnp.where(position < mine, longer, total)

    return lax.fori_loop(0, count - 1, hop, total)


def add_terms(earlier, later):
    return earlier + later


def neighbour_terms(fields, neighbours, weights):
    node_count = neighbours.shape[1]
    near_count = neighbours.shape[0]
    node_major = fields.T
    nearby = jnp.take(node_major, neighbours.reshape(-1), axis=0)
    nearby = nearby.reshape(near_count, node_count, fields.shape[0])
    differ = nearby - node_major[None, :node_count]
    return tuple(
        (
            jnp.einsum("knr,kn->rn", differ, weight, precision=lax.Precision.HIGHEST)
            for weight in weights
        )
    )


def local(
    velocity,
    density,
    elevation,
    grad_weights,
    lap_weights,
    coriolis,
    node_area,
    thickness,
    send_list,
    neighbours,
    bottom,
):
    level_count = density.shape[0]
    node_count = density.shape[1]
    half_slots = send_list.shape[1] // 2
    level_first = lax.axis_index("level") * level_count
    level_ids = level_first + jnp.arange(level_count, dtype=jnp.int32)
    wet_cells = (level_ids[:, None] < bottom[None, :]).astype(jnp.float32)
    at_floor = (level_ids[:, None] == bottom[None, :] - 1).astype(jnp.float32)
    wet_nodes = (bottom > 0).astype(jnp.float32)
    space_rank = lax.axis_index("space")
    space_count = lax.axis_size("space")
    slot_ids = jnp.arange(2 * half_slots, dtype=jnp.int32)
    halo_valid = jnp.where(
        slot_ids < half_slots, space_rank > 0, space_rank < space_count - 1
    ).astype(jnp.float32)
    valid_wide = jnp.concatenate([jnp.ones((node_count,), jnp.float32), halo_valid])
    valid_near = jnp.take(valid_wide, neighbours)
    weights = (grad_weights[0] * valid_near, grad_weights[1] * valid_near, lap_weights * valid_near)
    outgoing_ids = send_list[0]
    area_local = jnp.sum(node_area * wet_nodes)
    velocity = velocity * wet_cells[None]
    volume_terms = []
    for counter in range(STEPS):
        stacked = jnp.concatenate(
            [velocity.reshape(2 * level_count, node_count), density, elevation[None]], axis=0
        )
        outgoing = jnp.take(stacked.T, outgoing_ids, axis=0).T
        padded = extended_2(outgoing, (("space", 1),), half_slots)
        remote = jnp.concatenate([padded[:, :half_slots], padded[:, 3 * half_slots :]], axis=1)
        extended = jnp.concatenate([stacked, remote], axis=1)
        wide_velocity = extended[: 2 * level_count].reshape(2, level_count, extended.shape[1])
        wide_density = extended[2 * level_count : 3 * level_count]
        weighted = wide_density * thickness[:, None]
        own_total = jnp.sum(weighted, axis=0)
        transport_part = jnp.einsum(
            "cle,l->ce", wide_velocity, thickness, precision=lax.Precision.HIGHEST
        )
        above_sum = prefix(own_total, "level", add_terms, jnp.zeros_like(own_total))
        transport = lax.psum(transport_part, "level")
        pressure = buoyancy * (above_sum[None] + jnp.cumsum(weighted, axis=0) - 0.5 * weighted)
        fields = jnp.concatenate([extended, pressure, transport], axis=0)
        gradient_east, gradient_north, laplace = neighbour_terms(fields, neighbours, weights)
        elev_row = 3 * level_count
        press_first = 3 * level_count + 1
        flow_row = 4 * level_count + 1
        diverge = gradient_east[flow_row] + gradient_north[flow_row + 1]
        volume_term = jnp.sum(node_area * wet_nodes * diverge)
        new_elevation = elevation - time_step * wet_nodes * diverge
        volume_terms.append(volume_term)
        east_speed = velocity[0]
        north_speed = velocity[1]
        push_east = (
            -gradient_east[elev_row][None]
            - gradient_east[press_first : press_first + level_count]
            + coriolis[None] * north_speed
            + laplace[:level_count]
            - drag_rate * at_floor * east_speed
        )
        push_north = (
            -gradient_north[elev_row][None]
            - gradient_north[press_first : press_first + level_count]
            - coriolis[None] * east_speed
            + laplace[level_count : 2 * level_count]
            - drag_rate * at_floor * north_speed
        )
        density = density + time_step * (
            laplace[2 * level_count : 3 * level_count]
            - east_speed * gradient_east[2 * level_count : 3 * level_count]
            - north_speed * gradient_north[2 * level_count : 3 * level_count]
        )
        velocity = wet_cells[None] * (velocity + time_step * jnp.stack([push_east, push_north]))
        elevation = new_elevation
    summed, area_total = lax.psum((jnp.stack(volume_terms), area_local), "space")
    drifts = summed / area_total
    elevation = elevation + time_step * jnp.sum(drifts)
    return (velocity, density, elevation, drifts.astype(jnp.float32))


def solution(mesh):
    return jax.shard_map(
        local,
        mesh=mesh,
        in_specs=(
            P(None, "level", "space"),
            P("level", "space"),
            P("space"),
            P(None, None, "space"),
            P(None, "space"),
            P("space"),
            P("space"),
            P("level"),
            P("space", None),
            P(None, "space"),
            P("space"),
        ),
        out_specs=(P(None, "level", "space"), P("level", "space"), P("space"), P()),
        check_vma=False,
    )
```

profile of v0, /device:TPU:0, one launch (start us, length us, event | category | flops | bytes accessed | tf_op | source)
XLA Modules:
  0.0 274.5 jit_solution(15536687425961770250)
XLA Ops:
  5.5 4.9 %collective-permute-start = (f32[25,128]{0,1:T(8,128)S(1)}, f32[25,128]{0,1:T(8,128)S(1)}, u32[]{:S(2)}, u32[]{:S(2)}) collective-permute-start(f32[25,128]{0,1:T(8,128)S(1)} %get-tuple-element.135), channel_id=1, source_target_pairs={{0,2},{2,4},{4,6},{6,8},{8,10},{10,12},{12,14},{14,16},{16,18},{18... | collective-permute-start | bytes 38408 | tf_op jit(solution)/shard_map/ppermute | solution.py:21
  14.2 34.3 %gather_fusion = f32[6144]{0:T(1024)S(1)} fusion(f32[1280]{0:T(1024)S(1)} %pad_convert_fusion, s32[6144]{0:T(1024)S(1)} %broadcast_clamp_fusion), kind=kCustom, calls=%fused_computation.8 | custom fusion | bytes 73728 | tf_op jit(solution)/shard_map/jit(_take)/gather | solution.py:86
  51.0 3.3 %psum.42 = f32[2,1280]{1,0:T(2,128)S(1)} all-reduce(f32[2,1280]{1,0:T(2,128)S(1)} %bitcast.280), channel_id=1, replica_groups=mesh['space'=16,'level'=2] {'level'}, use_global_device_ids=true, to_apply=%region_2.4 | all-reduce | flops 2560 | bytes 20480 | tf_op jit(solution)/shard_map/psum | solution.py:108
  54.7 20.9 %gather_fusion.2 = f32[6144,35]{1,0:T(8,128)} fusion(f32[1280,35]{1,0:T(8,128)S(1)} %bitcast.231, s32[6144]{0:T(1024)S(1)} %fusion.68), kind=kCustom, calls=%fused_computation.1.clone | custom fusion | bytes 1744896 | tf_op jit(solution)/shard_map/jit(_take)/gather | solution.py:47
  75.6 4.7 %broadcast_select_fusion.3 = f32[6144,35]{1,0:T(8,128)S(1)} fusion(f32[6144,35]{1,0:T(8,128)} %gather_fusion.2, pred[6144]{0:T(1024)(128)(4,1)S(1)} %compare_and_fusion), kind=kLoop, calls=%fused_computation.24 | loop fusion | flops 215040 | bytes 1726464 | tf_op jit(solution)/shard_map/jit(_take)/select_n | solution.py:47
  80.3 3.2 %multiply_reduce_fusion.11 = (f32[1024,35]{1,0:T(8,128)S(1)}, f32[1024,35]{1,0:T(8,128)S(1)}, f32[1024,35]{1,0:T(8,128)S(1)}) fusion(f32[6,1024,35]{2,1,0:T(8,128)S(1)} %bitcast.237, f32[1024,6]{0,1:T(8,128)S(1)} %get-tuple-element.139, f32[1024,35]{1,0:T(8,128)S(1)} %slice.329, f32[1024,6]{0,1:T(8,128)S(1)} %get-tuple-element.138, ...), kind=kLoop, calls=%fused_computation.20 | loop fusion | flops 1397760 | bytes 1507328
  85.4 4.6 %collective-permute-start.2 = (f32[25,128]{0,1:T(8,128)S(1)}, f32[25,128]{0,1:T(8,128)S(1)}, u32[]{:S(2)}, u32[]{:S(2)}) collective-permute-start(f32[25,128]{0,1:T(8,128)S(1)} %get-tuple-element.133), channel_id=1, source_target_pairs={{0,2},{2,4},{4,6},{6,8},{8,10},{10,12},{12,14},{14,16},{16,18},{18... | collective-permute-start | bytes 38408 | tf_op jit(solution)/shard_map/ppermute | solution.py:21
  91.9 4.7 %collective-permute-done.3 = f32[25,128]{0,1:T(8,128)S(1)} collective-permute-done((f32[25,128]{0,1:T(8,128)S(1)}, f32[25,128]{0,1:T(8,128)S(1)}, u32[]{:S(2)}, u32[]{:S(2)}) %collective-permute-start.3) | collective-permute-done | bytes 12832 | tf_op jit(solution)/shard_map/ppermute | solution.py:22
  98.8 3.3 %psum.43 = f32[2,1280]{1,0:T(2,128)S(1)} all-reduce(f32[2,1280]{1,0:T(2,128)S(1)} %bitcast.281), channel_id=1, replica_groups=mesh['space'=16,'level'=2] {'level'}, use_global_device_ids=true, to_apply=%region_5.8 | all-reduce | flops 2560 | bytes 20480 | tf_op jit(solution)/shard_map/psum | solution.py:108
  102.4 20.9 %gather_fusion.4 = f32[6144,35]{1,0:T(8,128)} fusion(f32[1280,35]{1,0:T(8,128)S(1)} %bitcast.232, s32[6144]{0:T(1024)S(1)} %fusion.68), kind=kCustom, calls=%fused_computation.5.clone | custom fusion | bytes 1744896 | tf_op jit(solution)/shard_map/jit(_take)/gather | solution.py:47
  123.4 4.7 %broadcast_select_fusion.2 = f32[6144,35]{1,0:T(8,128)S(1)} fusion(f32[6144,35]{1,0:T(8,128)} %gather_fusion.4, pred[6144]{0:T(1024)(128)(4,1)S(1)} %compare_and_fusion), kind=kLoop, calls=%fused_computation.23 | loop fusion | flops 215040 | bytes 1726464 | tf_op jit(solution)/shard_map/jit(_take)/select_n | solution.py:47
  133.1 4.7 %collective-permute-start.4 = (f32[25,128]{0,1:T(8,128)S(1)}, f32[25,128]{0,1:T(8,128)S(1)}, u32[]{:S(2)}, u32[]{:S(2)}) collective-permute-start(f32[25,128]{0,1:T(8,128)S(1)} %get-tuple-element.131), channel_id=1, source_target_pairs={{0,2},{2,4},{4,6},{6,8},{8,10},{10,12},{12,14},{14,16},{16,18},{18... | collective-permute-start | bytes 38408 | tf_op jit(solution)/shard_map/ppermute | solution.py:21
  139.8 4.2 %collective-permute-done.5 = f32[25,128]{0,1:T(8,128)S(1)} collective-permute-done((f32[25,128]{0,1:T(8,128)S(1)}, f32[25,128]{0,1:T(8,128)S(1)}, u32[]{:S(2)}, u32[]{:S(2)}) %collective-permute-start.5) | collective-permute-done | bytes 12832 | tf_op jit(solution)/shard_map/ppermute | solution.py:22
  146.3 3.3 %psum.44 = f32[2,1280]{1,0:T(2,128)S(1)} all-reduce(f32[2,1280]{1,0:T(2,128)S(1)} %bitcast.282), channel_id=1, replica_groups=mesh['space'=16,'level'=2] {'level'}, use_global_device_ids=true, to_apply=%region_8.11 | all-reduce | flops 2560 | bytes 20480 | tf_op jit(solution)/shard_map/psum | solution.py:108
  149.9 20.9 %gather_fusion.6 = f32[6144,35]{1,0:T(8,128)} fusion(f32[1280,35]{1,0:T(8,128)S(1)} %bitcast.234, s32[6144]{0:T(1024)S(1)} %fusion.68), kind=kCustom, calls=%fused_computation.6.clone | custom fusion | bytes 1744896 | tf_op jit(solution)/shard_map/jit(_take)/gather | solution.py:47
  170.8 4.7 %broadcast_select_fusion.1 = f32[6144,35]{1,0:T(8,128)S(1)} fusion(f32[6144,35]{1,0:T(8,128)} %gather_fusion.6, pred[6144]{0:T(1024)(128)(4,1)S(1)} %compare_and_fusion), kind=kLoop, calls=%fused_computation.22 | loop fusion | flops 215040 | bytes 1726464 | tf_op jit(solution)/shard_map/jit(_take)/select_n | solution.py:47
  175.5 3.2 %multiply_reduce_fusion.5 = (f32[1024,35]{1,0:T(8,128)S(1)}, f32[1024,35]{1,0:T(8,128)S(1)}, f32[1024,35]{1,0:T(8,128)S(1)}) fusion(f32[6,1024,35]{2,1,0:T(8,128)S(1)} %bitcast.239, f32[1024,6]{0,1:T(8,128)S(1)} %get-tuple-element.139, f32[1024,35]{1,0:T(8,128)S(1)} %slice.363, f32[1024,6]{0,1:T(8,128)S(1)} %get-tuple-element.138, ...), kind=kLoop, calls=%fused_computation.14 | loop fusion | flops 1397760 | bytes 1507328
  180.5 4.8 %collective-permute-start.6 = (f32[25,128]{0,1:T(8,128)S(1)}, f32[25,128]{0,1:T(8,128)S(1)}, u32[]{:S(2)}, u32[]{:S(2)}) collective-permute-start(f32[25,128]{0,1:T(8,128)S(1)} %get-tuple-element.129), channel_id=1, source_target_pairs={{0,2},{2,4},{4,6},{6,8},{8,10},{10,12},{12,14},{14,16},{16,18},{18... | collective-permute-start | bytes 38408 | tf_op jit(solution)/shard_map/ppermute | solution.py:21
  187.2 4.2 %collective-permute-done.7 = f32[25,128]{0,1:T(8,128)S(1)} collective-permute-done((f32[25,128]{0,1:T(8,128)S(1)}, f32[25,128]{0,1:T(8,128)S(1)}, u32[]{:S(2)}, u32[]{:S(2)}) %collective-permute-start.7) | collective-permute-done | bytes 12832 | tf_op jit(solution)/shard_map/ppermute | solution.py:22
  193.8 3.3 %psum.45 = f32[2,1280]{1,0:T(2,128)S(1)} all-reduce(f32[2,1280]{1,0:T(2,128)S(1)} %bitcast.283), channel_id=1, replica_groups=mesh['space'=16,'level'=2] {'level'}, use_global_device_ids=true, to_apply=%region_11.14 | all-reduce | flops 2560 | bytes 20480 | tf_op jit(solution)/shard_map/psum | solution.py:108
  197.3 20.9 %gather_fusion.8 = f32[6144,35]{1,0:T(8,128)} fusion(f32[1280,35]{1,0:T(8,128)S(1)} %bitcast.228, s32[6144]{0:T(1024)S(1)} %fusion.68), kind=kCustom, calls=%fused_computation.7.clone | custom fusion | bytes 1744896 | tf_op jit(solution)/shard_map/jit(_take)/gather | solution.py:47
  218.3 4.7 %broadcast_select_fusion = f32[6144,35]{1,0:T(8,128)S(1)} fusion(f32[6144,35]{1,0:T(8,128)} %gather_fusion.8, pred[6144]{0:T(1024)(128)(4,1)S(1)} %compare_and_fusion), kind=kLoop, calls=%fused_computation.21 | loop fusion | flops 215040 | bytes 1726464 | tf_op jit(solution)/shard_map/jit(_take)/select_n | solution.py:47
  223.0 3.2 %multiply_reduce_fusion.2 = (f32[1024,35]{1,0:T(8,128)S(1)}, f32[1024,35]{1,0:T(8,128)S(1)}, f32[1024,35]{1,0:T(8,128)S(1)}) fusion(f32[6,1024,35]{2,1,0:T(8,128)S(1)} %bitcast.236, f32[1024,6]{0,1:T(8,128)S(1)} %get-tuple-element.139, f32[1024,35]{1,0:T(8,128)S(1)} %slice.380, f32[1024,6]{0,1:T(8,128)S(1)} %get-tuple-element.138, ...), kind=kLoop, calls=%fused_computation.11 | loop fusion | flops 1397760 | bytes 1507328
  230.0 40.0 %all-reduce.1 = (f32[4]{0:T(128)S(1)}, f32[]{:T(128)}) all-reduce(f32[4]{0:T(128)S(1)} %pad_maximum_fusion.36, f32[]{:T(128)} %get-tuple-element.86), channel_id=1, replica_groups=mesh['space'=16,'level'=2] {'space'}, use_global_device_ids=true, to_apply=%region_16.19 | all-reduce | flops 5 | bytes 40 | tf_op jit(solution)/shard_map/psum | solution.py:142
  (155 shorter events, 41.2 us)
Async XLA Ops:
  5.5 43.2 %collective-permute-start = (f32[25,128]{0,1:T(8,128)S(1)}, f32[25,128]{0,1:T(8,128)S(1)}, u32[]{:S(2)}, u32[]{:S(2)}) collective-permute-start(f32[25,128]{0,1:T(8,128)S(1)} %get-tuple-element.135), channel_id=1, source_target_pairs={{0,2},{2,4},{4,6},{6,8},{8,10},{10,12},{12,14},{14,16},{16,18},{18... | collective-permute-start | bytes 38408 | tf_op jit(solution)/shard_map/ppermute | solution.py:21
  10.4 38.4 %collective-permute-start.1 = (f32[25,128]{0,1:T(8,128)S(1)}, f32[25,128]{0,1:T(8,128)S(1)}, u32[]{:S(2)}, u32[]{:S(2)}) collective-permute-start(f32[25,128]{0,1:T(8,128)S(1)} %get-tuple-element.136), channel_id=1, source_target_pairs={{2,0},{4,2},{6,4},{8,6},{10,8},{12,10},{14,12},{16,14},{18,16},{20... | collective-permute-start | bytes 38408 | tf_op jit(solution)/shard_map/ppermute | solution.py:22
  14.1 34.4 %copy-start.5 = (f32[2,6,1024]{2,0,1:T(2,128)S(1)}, f32[2,6,1024]{2,0,1:T(2,128)}, u32[]{:S(2)}) copy-start(f32[2,6,1024]{2,0,1:T(2,128)} %param.18) | copy-start | bytes 147460
  14.1 34.4 %copy-start.2 = (s32[6,1024]{1,0:T(8,128)S(1)}, s32[6,1024]{1,0:T(8,128)}, u32[]{:S(2)}) copy-start(s32[6,1024]{1,0:T(8,128)} %param.24) | copy-start | bytes 73732
  14.2 34.4 %copy-start.7 = (f32[6,1024]{1,0:T(8,128)S(1)}, f32[6,1024]{1,0:T(8,128)}, u32[]{:S(2)}) copy-start(f32[6,1024]{1,0:T(8,128)} %param.19) | copy-start | bytes 73732
  14.2 34.5 %copy-start.6 = (s32[1024]{0:T(1024)S(1)}, s32[1024]{0:T(1024)}, u32[]{:S(2)}) copy-start(s32[1024]{0:T(1024)} %param.25) | copy-start | bytes 12292
  14.2 34.6 %copy-start.1 = (f32[8,1024]{1,0:T(8,128)S(1)}, f32[8,1024]{1,0:T(8,128)}, u32[]{:S(2)}) copy-start(f32[8,1024]{1,0:T(8,128)} %param.16) | copy-start | bytes 98308
  14.2 34.6 %copy-start.4 = (f32[1024]{0:T(1024)S(1)}, f32[1024]{0:T(1024)}, u32[]{:S(2)}) copy-start(f32[1024]{0:T(1024)} %param.17) | copy-start | bytes 12292
  14.2 34.6 %copy-start.8 = (f32[8]{0:T(128)S(1)}, f32[8]{0:T(128)}, u32[]{:S(2)}) copy-start(f32[8]{0:T(128)} %param.22) | copy-start | bytes 100
  80.3 3.8 %copy-start.3 = (f32[1024]{0:T(1024)S(1)}, f32[1024]{0:T(1024)}, u32[]{:S(2)}) copy-start(f32[1024]{0:T(1024)} %param.20) | copy-start | bytes 12292
  80.3 3.9 %copy-start = (f32[2,8,1024]{2,1,0:T(8,128)S(1)}, f32[2,8,1024]{2,1,0:T(8,128)}, u32[]{:S(2)}) copy-start(f32[2,8,1024]{2,1,0:T(8,128)} %param.15) | copy-start | bytes 196612
  85.4 6.4 %collective-permute-start.2 = (f32[25,128]{0,1:T(8,128)S(1)}, f32[25,128]{0,1:T(8,128)S(1)}, u32[]{:S(2)}, u32[]{:S(2)}) collective-permute-start(f32[25,128]{0,1:T(8,128)S(1)} %get-tuple-element.133), channel_id=1, source_target_pairs={{0,2},{2,4},{4,6},{6,8},{8,10},{10,12},{12,14},{14,16},{16,18},{18... | collective-permute-start | bytes 38408 | tf_op jit(solution)/shard_map/ppermute | solution.py:21
  89.9 6.6 %collective-permute-start.3 = (f32[25,128]{0,1:T(8,128)S(1)}, f32[25,128]{0,1:T(8,128)S(1)}, u32[]{:S(2)}, u32[]{:S(2)}) collective-permute-start(f32[25,128]{0,1:T(8,128)S(1)} %get-tuple-element.134), channel_id=1, source_target_pairs={{2,0},{4,2},{6,4},{8,6},{10,8},{12,10},{14,12},{16,14},{18,16},{20... | collective-permute-start | bytes 38408 | tf_op jit(solution)/shard_map/ppermute | solution.py:22
  133.1 6.6 %collective-permute-start.4 = (f32[25,128]{0,1:T(8,128)S(1)}, f32[25,128]{0,1:T(8,128)S(1)}, u32[]{:S(2)}, u32[]{:S(2)}) collective-permute-start(f32[25,128]{0,1:T(8,128)S(1)} %get-tuple-element.131), channel_id=1, source_target_pairs={{0,2},{2,4},{4,6},{6,8},{8,10},{10,12},{12,14},{14,16},{16,18},{18... | collective-permute-start | bytes 38408 | tf_op jit(solution)/shard_map/ppermute | solution.py:21
  137.8 6.2 %collective-permute-start.5 = (f32[25,128]{0,1:T(8,128)S(1)}, f32[25,128]{0,1:T(8,128)S(1)}, u32[]{:S(2)}, u32[]{:S(2)}) collective-permute-start(f32[25,128]{0,1:T(8,128)S(1)} %get-tuple-element.132), channel_id=1, source_target_pairs={{2,0},{4,2},{6,4},{8,6},{10,8},{12,10},{14,12},{16,14},{18,16},{20... | collective-permute-start | bytes 38408 | tf_op jit(solution)/shard_map/ppermute | solution.py:22
  180.5 6.6 %collective-permute-start.6 = (f32[25,128]{0,1:T(8,128)S(1)}, f32[25,128]{0,1:T(8,128)S(1)}, u32[]{:S(2)}, u32[]{:S(2)}) collective-permute-start(f32[25,128]{0,1:T(8,128)S(1)} %get-tuple-element.129), channel_id=1, source_target_pairs={{0,2},{2,4},{4,6},{6,8},{8,10},{10,12},{12,14},{14,16},{16,18},{18... | collective-permute-start | bytes 38408 | tf_op jit(solution)/shard_map/ppermute | solution.py:21
  185.3 6.2 %collective-permute-start.7 = (f32[25,128]{0,1:T(8,128)S(1)}, f32[25,128]{0,1:T(8,128)S(1)}, u32[]{:S(2)}, u32[]{:S(2)}) collective-permute-start(f32[25,128]{0,1:T(8,128)S(1)} %get-tuple-element.130), channel_id=1, source_target_pairs={{2,0},{4,2},{6,4},{8,6},{10,8},{12,10},{14,12},{16,14},{18,16},{20... | collective-permute-start | bytes 38408 | tf_op jit(solution)/shard_map/ppermute | solution.py:22
  223.0 3.6 %copy-start.9 = (f32[1024]{0:T(1024)S(1)}, f32[1024]{0:T(1024)}, u32[]{:S(2)}) copy-start(f32[1024]{0:T(1024)} %param.21) | copy-start | bytes 12292
where the time goes:
time: 276 us; the launch traced here: 275 us
  local copies, waits for them, and re-layouts  127 us (46%)
  blocking collectives  60.4 us (22%)
  other arithmetic  45.6 us (17%)
  starting transfers between devices  24.1 us (9%)
  waiting for transfers between devices  14.7 us (5%)
    gather x4, local copies, waits for them, and re-layouts, neighbour_terms(): nearby = jnp.take(node_major, neighbours.reshape(-1), axis=0)  83.6 us
    psum x1, blocking collectives, local(): lax.psum((jnp.stack(volume_terms), area_local), 'space')  40 us
    gather x2, local copies, waits for them, and re-layouts, local(): valid_near = jnp.take(valid_wide, neighbours)  34.3 us
    ppermute x4, starting transfers between devices, extended_2(): before = lax.ppermute(last, axis, up)  18.9 us
    select_n x4, other arithmetic, neighbour_terms(): nearby = jnp.take(node_major, neighbours.reshape(-1), axis=0)  18.7 us
    psum x4, blocking collectives, local(): transport = lax.psum(transport_part, 'level')  13.2 us
    ppermute x4, waiting for transfers between devices, extended_2(): after = lax.ppermute(first, axis, down)  13.1 us
    unnamed x5, other arithmetic  12.7 us
  transfers between devices with their start and end apart: 8, of which 6 were waited for; matrix products, arithmetic and copies ran while one was open for 14% of the time, Pallas kernels for 0%

commit v1 on v0

v1 whole, which is shorter than its diff:
```python
import jax
import jax.numpy as jnp
from jax import lax
from jax.experimental import pallas as pl
from jax.experimental.pallas import tpu as pltpu
from jax.sharding import PartitionSpec as P

STEPS = 4

time_step = 0.1
buoyancy = 0.5
drag_rate = 0.5

LANES = 128
SUBS = 8


def lane_gather(source, lane):
    return lax.gather(
        source,
        lane[..., None],
        lax.GatherDimensionNumbers(
            offset_dims=(),
            collapsed_slice_dims=(1,),
            start_index_map=(1,),
            operand_batching_dims=(0,),
            start_indices_batching_dims=(0,),
        ),
        slice_sizes=(1, 1),
        mode=lax.GatherScatterMode.PROMISE_IN_BOUNDS,
    )


def spread(row, rows=SUBS):
    return jnp.broadcast_to(row, (rows, row.shape[1]))


def level_prefix(value):
    sub = lax.broadcasted_iota(jnp.int32, (SUBS, LANES), 0)
    out, carry = [], None
    for block in value:
        shift = 1
        while shift < SUBS:
            block = block + jnp.where(sub >= shift, pltpu.roll(block, shift, 0), 0.0)
            shift *= 2
        if carry is not None:
            block = block + carry
        carry = spread(block[SUBS - 1 :])
        out.append(block)
    return out


def pick(sources, lane, block):
    out = None
    for number, rows in enumerate(sources):
        here = [lane_gather(row(), lane) for row in rows]
        if out is None:
            out = here
        else:
            match = block == number
            out = [jnp.where(match, new, old) for new, old in zip(here, out)]
    return out


def send_out(state, eta, send, outgoing):
    rows, node_count = state.shape
    half = send.shape[1] // 2
    for side in range(2):
        for chunk in range(half // LANES):
            first = side * half + chunk * LANES
            ids = spread(send[0:1, first : first + LANES])
            sources = []
            for number in range(node_count // LANES):
                cols = slice(number * LANES, (number + 1) * LANES)
                own = [
                    lambda g=g, cols=cols: state[g : g + SUBS, cols]
                    for g in range(0, rows, SUBS)
                ]
                own.append(lambda cols=cols: spread(eta[0:1, cols]))
                sources.append(own)
            found = pick(sources, ids & (LANES - 1), ids >> 7)
            for g, block in enumerate(found):
                outgoing[
                    side, g * SUBS : (g + 1) * SUBS, chunk * LANES : (chunk + 1) * LANES
                ] = block


def begin_kernel(parts, eta, bottom, node_area, send, state, outgoing, volume):
    shards, held, width = parts.shape
    fields, node_count = 3, eta.shape[1]
    level_count = shards * held
    area = jnp.where(bottom[0:1, :] > 0, node_area[0:1, :], 0.0)
    area = sum(area[:, i : i + LANES] for i in range(0, node_count, LANES))
    sub = lax.broadcasted_iota(jnp.int32, (SUBS, LANES), 0)
    volume[...] = jnp.where(sub == STEPS, spread(area), 0.0)
    for shard in range(shards):
        ids = lax.broadcasted_iota(jnp.int32, (held, node_count), 0) + shard * held
        wet = ids < jnp.broadcast_to(bottom[0:1, :], (held, node_count))
        for field in range(fields):
            value = parts[shard, :, field * node_count : (field + 1) * node_count]
            if field < 2:
                value = jnp.where(wet, value, 0.0)
            first = field * level_count + shard * held
            state[first : first + held, :] = value
    send_out(state, eta, send, outgoing)


def step_kernel(
    edges,
    volume_in,
    state,
    eta,
    first_halo,
    second_halo,
    neighbours,
    weights,
    coriolis,
    node_area,
    bottom,
    thickness,
    send,
    new_state,
    new_eta,
    outgoing,
    volume,
    *,
    near_count,
    step,
):
    rows, node_count = state.shape
    half = first_halo.shape[1]
    level_count = rows // 3
    groups = level_count // SUBS
    slots = (node_count, node_count + half)
    first_ok, second_ok = edges[0], edges[1]

    def source_blocks():
        for ref, width in ((state, node_count), (first_halo, half), (second_halo, half)):
            for number in range(width // LANES):
                cols = slice(number * LANES, (number + 1) * LANES)
                yield ref, cols

    eta_sources, state_sources = [], []
    for ref, cols in source_blocks():
        eta_ref, eta_row = (eta, 0) if ref is state else (ref, rows)
        eta_sources.append(
            [lambda r=eta_ref, i=eta_row, c=cols: spread(r[i : i + 1, c])]
        )
        state_sources.append(
            [lambda r=ref, g=g, c=cols: r[g : g + SUBS, c] for g in range(0, rows, SUBS)]
        )

    sub = lax.broadcasted_iota(jnp.int32, (SUBS, LANES), 0)

    def tile(number, total):
        cols = pl.ds(pl.multiple_of(number * LANES, LANES), LANES)
        ids = neighbours[:, cols]
        lanes, blocks = ids & (LANES - 1), ids >> 7
        valid = jnp.where(ids < slots[0], 1.0, jnp.where(ids < slots[1], first_ok, second_ok))
        east, north, smooth = (weights[i, :, cols] * valid for i in range(3))
        eta_here = eta[0:1, cols]
        (eta_near,) = pick(eta_sources, lanes, blocks)
        eta_differ = eta_near - spread(eta_here)
        slope_east = spread(jnp.sum(east * eta_differ, axis=0, keepdims=True))
        slope_north = spread(jnp.sum(north * eta_differ, axis=0, keepdims=True))

        own = [state[g : g + SUBS, cols] for g in range(0, rows, SUBS)]
        zero = jnp.zeros((SUBS, LANES), jnp.float32)
        lap = [zero] * (3 * groups)
        flow = [zero] * groups
        dense_east = [zero] * groups
        dense_north = [zero] * groups
        for k in range(near_count):
            found = pick(state_sources, spread(lanes[k : k + 1]), spread(blocks[k : k + 1]))
            e, n, w = (spread(x[k : k + 1]) for x in (east, north, smooth))
            differ = [near - here for near, here in zip(found, own)]
            for i, value in enumerate(differ):
                lap[i] = lap[i] + w * value
            for g in range(groups):
                flow[g] = flow[g] + (e * differ[g] + n * differ[groups + g])
                dense_east[g] = dense_east[g] + e * differ[2 * groups + g]
                dense_north[g] = dense_north[g] + n * differ[2 * groups + g]

        thick = [thickness[g * SUBS : (g + 1) * SUBS, :] for g in range(groups)]
        diverge = sum(thick[g] * flow[g] for g in range(groups))
        diverge = jnp.sum(diverge, axis=0, keepdims=True)
        depth = bottom[0:1, cols]
        wet_nodes = jnp.where(depth > 0, 1.0, 0.0)
        total = total + node_area[0:1, cols] * wet_nodes * diverge
        new_eta[0:1, cols] = eta_here - time_step * wet_nodes * diverge

        weighted_east = [t * x for t, x in zip(thick, dense_east)]
        weighted_north = [t * x for t, x in zip(thick, dense_north)]
        press_east = level_prefix(weighted_east)
        press_north = level_prefix(weighted_north)
        turn = spread(coriolis[0:1, cols])
        depth = spread(depth)
        for g in range(groups):
            u, v, rho = (own[f * groups + g] for f in range(3))
            level = sub + g * SUBS
            wet = level < depth
            drag = jnp.where(level == depth - 1, drag_rate, 0.0)
            push_east = (
                lap[g]
                - slope_east
                - buoyancy * (press_east[g] - 0.5 * weighted_east[g])
                + turn * v
                - drag * u
            )
            push_north = (
                lap[groups + g]
                - slope_north
                - buoyancy * (press_north[g] - 0.5 * weighted_north[g])
                - turn * u
                - drag * v
            )
            rho_new = rho + time_step * (
                lap[2 * groups + g] - u * dense_east[g] - v * dense_north[g]
            )
            u_new = jnp.where(wet, u + time_step * push_east, 0.0)
            v_new = jnp.where(wet, v + time_step * push_north, 0.0)
            for f, value in enumerate((u_new, v_new, rho_new)):
                first = (f * groups + g) * SUBS
                new_state[first : first + SUBS, cols] = value
        return total

    total = lax.fori_loop(
        0, node_count // LANES, tile, jnp.zeros((1, LANES), jnp.float32)
    )
    volume[...] = jnp.where(sub == step, spread(total), volume_in[...])
    send_out(new_state, new_eta, send, outgoing)


def vmem(count):
    return [pl.BlockSpec(memory_space=pltpu.VMEM)] * count


def shape(*dims):
    return jax.ShapeDtypeStruct(dims, jnp.float32)


def make_local(mesh):
    def local(
        velocity,
        density,
        elevation,
        grad_weights,
        lap_weights,
        coriolis,
        node_area,
        thickness,
        send_list,
        neighbours,
        bottom,
    ):
        held, node_count = density.shape
        near_count = neighbours.shape[0]
        half = send_list.shape[1] // 2
        shards = mesh.shape["level"]
        space_count = mesh.shape["space"]
        level_count = shards * held
        rows = 3 * level_count
        space_rank = lax.axis_index("space")
        level_rank = lax.axis_index("level")
        ends = space_count - 1
        rounds = [
            [(i, j if 0 <= j <= ends else i) for i, j in pairs]
            for pairs in (
                [(i, i ^ 1) for i in range(space_count)],
                [(i, ((i + 1) ^ 1) - 1) for i in range(space_count)],
            )
        ]
        even = space_rank % 2 == 0
        send = jnp.where(even, jnp.roll(send_list, half, axis=1), send_list)
        swapped = neighbours + jnp.where(neighbours < node_count + half, half, -half)
        near = jnp.where(even & (neighbours >= node_count), swapped, neighbours)
        low, high = space_rank > 0, space_rank < ends
        edges = jnp.stack([jnp.where(even, high, low), jnp.where(even, low, high)])
        edges = edges.astype(jnp.float32)

        thick = jnp.broadcast_to(thickness[:, None], (held, LANES))
        own = jnp.concatenate([velocity[0], velocity[1], density, thick], axis=1)
        parts = lax.all_gather(own, "level")
        thick = parts[:, :, 3 * node_count :].reshape(level_count, LANES)
        pad = -near_count % SUBS
        near = jnp.pad(near, ((0, pad), (0, 0)))
        weights = jnp.concatenate([grad_weights, lap_weights[None]], axis=0)
        weights = jnp.pad(weights, ((0, 0), (0, pad), (0, 0)))
        eta = elevation[None]
        depth = bottom[None]
        area = node_area[None]
        out_shape = shape(2, rows + SUBS, half)

        state, outgoing, volume = pl.pallas_call(
            begin_kernel,
            out_shape=(shape(rows, node_count), out_shape, shape(SUBS, LANES)),
            in_specs=vmem(5),
            out_specs=tuple(vmem(3)),
            name="begin",
        )(parts, eta, depth, area, send)

        for step in range(STEPS):
            halos = [lax.ppermute(outgoing[i], "space", rounds[i]) for i in range(2)]

            def body(*refs, step=step):
                step_kernel(*refs, near_count=near_count, step=step)

            state, eta, outgoing, volume = pl.pallas_call(
                body,
                out_shape=(
                    shape(rows, node_count),
                    shape(1, node_count),
                    out_shape,
                    shape(SUBS, LANES),
                ),
                in_specs=[pl.BlockSpec(memory_space=pltpu.SMEM)] + vmem(12),
                out_specs=tuple(vmem(4)),
                name="step",
            )(
                edges, volume, state, eta, *halos, near, weights,
                coriolis[None], area, depth, thick, send,
            )

        shared = jnp.broadcast_to(volume, (space_count,) + volume.shape)
        shared = lax.all_to_all(shared, "space", 0, 0)
        summed = jnp.sum(shared, axis=(0, 2))
        drifts = summed[:STEPS] / summed[STEPS]
        eta = eta[0] + time_step * jnp.sum(drifts)
        fields = state.reshape(3, level_count, node_count)
        mine = lax.dynamic_slice_in_dim(fields, level_rank * held, held, axis=1)
        return mine[:2], mine[2], eta, drifts

    return local


def solution(mesh):
    return jax.shard_map(
        make_local(mesh),
        mesh=mesh,
        in_specs=(
            P(None, "level", "space"),
            P("level", "space"),
            P("space"),
            P(None, None, "space"),
            P(None, "space"),
            P("space"),
            P("space"),
            P("level"),
            P("space", None),
            P(None, "space"),
            P("space"),
        ),
        out_specs=(P(None, "level", "space"), P("level", "space"), P("space"), P()),
        check_vma=False,
    )
```

time: 276 us -> 90.9 us (0.33)
  local copies, waits for them, and re-layouts: 127 us -> 13.6 us
  blocking collectives: 60.4 us -> 2.22 us
  other arithmetic: 45.6 us -> 4.35 us
  Pallas kernels: 0 us -> 25.6 us
  starting transfers between devices: 24.1 us -> 32.9 us
  waiting for transfers between devices: 14.7 us -> 9.83 us
    gather x10 -> x0, local copies, waits for them, and re-layouts: 121 us -> none  [the longest x4 83.6 us: neighbour_terms(): nearby = jnp.take(node_major, neighbours.reshape(-1), axis=0)]
    psum x5 -> x0, blocking collectives: 53.2 us -> none  [the longest x1 40 us: local(): lax.psum((jnp.stack(volume_terms), area_local), 'space')]
    pallas_call x0 -> x5, Pallas kernels: none -> 25.6 us  [the longest x4 23.9 us: local(): pl.pallas_call(body, out_shape=(shape(rows, node_count), shape(1, node_co...]
    select_n x11 -> x2, other arithmetic: 20.2 us -> 0.59 us  [the longest x1 0.57 us: local(): send = jnp.where(even, jnp.roll(send_list, half, axis=1), send_list)]
    unnamed x5 -> x0, other arithmetic: 12.7 us -> none
    all_to_all x0 -> x1, starting transfers between devices: none -> 12.6 us  [local(): shared = lax.all_to_all(shared, 'space', 0, 0)]
    ppermute x8, waiting for transfers between devices: 14.7 us -> 3.57 us  [local(): halos = [lax.ppermute(outgoing[i], 'space', rounds[i]) for i in range(2)]]
    all_to_all x0 -> x1, waiting for transfers between devices: none -> 6.26 us  [local(): shared = lax.all_to_all(shared, 'space', 0, 0)]
  transfers between devices with their start and end apart: 8 -> 9, of which waited for: 6 -> 4; matrix products, arithmetic and copies ran while one was open for 14% -> 5% of each run, Pallas kernels for 0% -> 0%
where the time goes in v1:
time: 90.9 us; the launch traced here: 89.9 us
  starting transfers between devices  32.9 us (36%)
  Pallas kernels  25.6 us (28%)
  local copies, waits for them, and re-layouts  13.6 us (15%)
  waiting for transfers between devices  9.83 us (11%)
  other arithmetic  4.35 us (5%)
  blocking collectives  2.22 us (2%)
  between operations  1.45 us (2%)
    pallas_call x4, Pallas kernels, local(): pl.pallas_call(body, out_shape=(shape(rows, node_count), shape(1, node_co...  23.9 us
    ppermute x8, starting transfers between devices, local(): halos = [lax.ppermute(outgoing[i], 'space', rounds[i]) for i in range(2)]  20.2 us
    all_to_all x1, starting transfers between devices, local(): shared = lax.all_to_all(shared, 'space', 0, 0)  12.6 us
    all_to_all x1, waiting for transfers between devices, local(): shared = lax.all_to_all(shared, 'space', 0, 0)  6.26 us
    unnamed x33, local copies, waits for them, and re-layouts  4.53 us
    ppermute x8, waiting for transfers between devices, local(): halos = [lax.ppermute(outgoing[i], 'space', rounds[i]) for i in range(2)]  3.57 us
    squeeze x4, local copies, waits for them, and re-layouts, local(): halos = [lax.ppermute(outgoing[i], 'space', rounds[i]) for i in range(2)]  3.08 us
    all_gather x1, blocking collectives, local(): parts = lax.all_gather(own, 'level')  2.22 us
  transfers between devices with their start and end apart: 9, of which 4 were waited for; matrix products, arithmetic and copies ran while one was open for 5% of the time, Pallas kernels for 0%

profile of v1, /device:TPU:0, one launch (start us, length us, event | category | flops | bytes accessed | tf_op | source)
XLA Modules:
  0.0 89.9 jit_solution(8009372731762898882)
XLA Ops:
  1.3 0.8 slice_bitcast_fusion.1
  2.9 2.2 %all-gather = f32[16,3200]{1,0:T(8,128)} all-gather(f32[8,3200]{1,0:T(8,128)S(1)} %pad_maximum_fusion), channel_id=2, replica_groups=mesh['space'=16,'level'=2] {'level'}, dimensions={0}, use_global_device_ids=true | all-gather | bytes 307200 | tf_op jit(solution)/shard_map/all_gather | solution.py:283
  5.7 1.8 %begin.1 = (f32[48,1024]{1,0:T(8,128)}, f32[2,56,128]{2,1,0:T(8,128)}, f32[8,128]{1,0:T(8,128)}) custom-call(f32[2,8,3200]{2,1,0:T(8,128)} %bitcast.35, f32[1,1024]{1,0:T(1,128)} %bitcast.54, s32[1,1024]{1,0:T(1,128)} %bitcast.37, f32[1,1024]{1,0:T(1,128)} %bitcast.42, s32[1,256]{1,0:T(1,128)} %broadcast_select_fusion.send.refs_12_), custom_call_target="tpu_custom_call" | custom-call | tf_op jit(solution)/shard_map/begin/pallas_call | solution.py:294
  7.4 0.8 slice_bitcast_fusion.8
  8.2 2.8 %collective-permute-start = (f32[56,128]{1,0:T(8,128)S(1)}, f32[56,128]{1,0:T(8,128)S(1)}, u32[]{:S(2)}, u32[]{:S(2)}) collective-permute-start(f32[56,128]{1,0:T(8,128)S(1)} %get-tuple-element.51), channel_id=1, source_target_pairs={{0,2},{2,0},{4,6},{6,4},{8,10},{10,8},{12,14},{14,12},{16,18},{18,... | collective-permute-start | bytes 86024 | tf_op jit(solution)/shard_map/ppermute | solution.py:303
  11.7 1.3 %slice_bitcast_fusion.10.refs_11_ = f32[16,128]{1,0:T(8,128)} fusion(f32[2,8,3200]{2,1,0:T(8,128)} %bitcast.36), kind=kLoop, calls=%fused_computation.15 | loop fusion | bytes 16384 | tf_op jit(solution)/shard_map/reshape | solution.py:284
  13.1 0.7 copy-done.4
  16.3 6.0 %step.4 = (f32[48,1024]{1,0:T(8,128)}, f32[1,1024]{1,0:T(1,128)}, f32[2,56,128]{2,1,0:T(8,128)}, f32[8,128]{1,0:T(8,128)}) custom-call(f32[2]{0:T(128)} %add_convert_fusion.refs_0_, f32[8,128]{1,0:T(8,128)} %get-tuple-element.22.refs_1_, f32[48,1024]{1,0:T(8,128)} %get-tuple-element.23.refs_2_, f32[1,1024]{1,0:T(1,128)} %bitcast.55, f32[56,128]{1,0:T(8,128)} %copy-done.6, ...), custom_call_target="tpu_custom_call" | custom-call | tf_op jit(solution)/shard_map/step/pallas_call | solution.py:308
  22.3 0.8 slice_bitcast_fusion.6
  23.1 4.2 %collective-permute-start.2 = (f32[56,128]{1,0:T(8,128)S(1)}, f32[56,128]{1,0:T(8,128)S(1)}, u32[]{:S(2)}, u32[]{:S(2)}) collective-permute-start(f32[56,128]{1,0:T(8,128)S(1)} %get-tuple-element.49), channel_id=1, source_target_pairs={{0,2},{2,0},{4,6},{6,4},{8,10},{10,8},{12,14},{14,12},{16,18},{18,... | collective-permute-start | bytes 86024 | tf_op jit(solution)/shard_map/ppermute | solution.py:303
  28.0 1.2 %collective-permute-done.2.refs_4_ = f32[56,128]{1,0:T(8,128)S(1)} collective-permute-done((f32[56,128]{1,0:T(8,128)S(1)}, f32[56,128]{1,0:T(8,128)S(1)}, u32[]{:S(2)}, u32[]{:S(2)}) %collective-permute-start.2) | collective-permute-done | bytes 28704 | tf_op jit(solution)/shard_map/ppermute | solution.py:303
  29.8 6.0 %step.5 = (f32[48,1024]{1,0:T(8,128)}, f32[1,1024]{1,0:T(1,128)}, f32[2,56,128]{2,1,0:T(8,128)}, f32[8,128]{1,0:T(8,128)}) custom-call(f32[2]{0:T(128)} %add_convert_fusion.refs_0_, f32[8,128]{1,0:T(8,128)} %get-tuple-element.25.refs_1_, f32[48,1024]{1,0:T(8,128)} %get-tuple-element.26.refs_2_, f32[1,1024]{1,0:T(1,128)} %get-tuple-element.27.refs_3_, ...), custom_call_target="tpu_custom_call" | custom-call | tf_op jit(solution)/shard_map/step/pallas_call | solution.py:308
  35.7 0.8 slice_bitcast_fusion.4
  36.5 4.9 %collective-permute-start.4 = (f32[56,128]{1,0:T(8,128)S(1)}, f32[56,128]{1,0:T(8,128)S(1)}, u32[]{:S(2)}, u32[]{:S(2)}) collective-permute-start(f32[56,128]{1,0:T(8,128)S(1)} %get-tuple-element.47), channel_id=1, source_target_pairs={{0,2},{2,0},{4,6},{6,4},{8,10},{10,8},{12,14},{14,12},{16,18},{18,... | collective-permute-start | bytes 86024 | tf_op jit(solution)/shard_map/ppermute | solution.py:303
  42.0 1.2 %collective-permute-done.4.refs_4_ = f32[56,128]{1,0:T(8,128)S(1)} collective-permute-done((f32[56,128]{1,0:T(8,128)S(1)}, f32[56,128]{1,0:T(8,128)S(1)}, u32[]{:S(2)}, u32[]{:S(2)}) %collective-permute-start.4) | collective-permute-done | bytes 28704 | tf_op jit(solution)/shard_map/ppermute | solution.py:303
  43.8 6.0 %step.6 = (f32[48,1024]{1,0:T(8,128)}, f32[1,1024]{1,0:T(1,128)}, f32[2,56,128]{2,1,0:T(8,128)}, f32[8,128]{1,0:T(8,128)}) custom-call(f32[2]{0:T(128)} %add_convert_fusion.refs_0_, f32[8,128]{1,0:T(8,128)} %get-tuple-element.29.refs_1_, f32[48,1024]{1,0:T(8,128)} %get-tuple-element.30.refs_2_, f32[1,1024]{1,0:T(1,128)} %get-tuple-element.31.refs_3_, ...), custom_call_target="tpu_custom_call" | custom-call | tf_op jit(solution)/shard_map/step/pallas_call | solution.py:308
  49.8 0.8 slice_bitcast_fusion.2
  50.6 5.7 %collective-permute-start.6 = (f32[56,128]{1,0:T(8,128)S(1)}, f32[56,128]{1,0:T(8,128)S(1)}, u32[]{:S(2)}, u32[]{:S(2)}) collective-permute-start(f32[56,128]{1,0:T(8,128)S(1)} %get-tuple-element.45), channel_id=1, source_target_pairs={{0,2},{2,0},{4,6},{6,4},{8,10},{10,8},{12,14},{14,12},{16,18},{18,... | collective-permute-start | bytes 86024 | tf_op jit(solution)/shard_map/ppermute | solution.py:303
  56.9 1.2 %collective-permute-done.6.refs_4_ = f32[56,128]{1,0:T(8,128)S(1)} collective-permute-done((f32[56,128]{1,0:T(8,128)S(1)}, f32[56,128]{1,0:T(8,128)S(1)}, u32[]{:S(2)}, u32[]{:S(2)}) %collective-permute-start.6) | collective-permute-done | bytes 28704 | tf_op jit(solution)/shard_map/ppermute | solution.py:303
  58.7 6.0 %step.7 = (f32[48,1024]{1,0:T(8,128)}, f32[1,1024]{1,0:T(1,128)}, f32[2,56,128]{2,1,0:T(8,128)}, f32[8,128]{1,0:T(8,128)}) custom-call(f32[2]{0:T(128)} %add_convert_fusion.refs_0_, f32[8,128]{1,0:T(8,128)} %get-tuple-element.33.refs_1_, f32[48,1024]{1,0:T(8,128)} %get-tuple-element.34.refs_2_, f32[1,1024]{1,0:T(1,128)} %get-tuple-element.35.refs_3_, ...), custom_call_target="tpu_custom_call" | custom-call | tf_op jit(solution)/shard_map/step/pallas_call | solution.py:308
  64.7 1.4 %broadcast_in_dim.43 = f32[16,8,128]{2,1,0:T(8,128)} broadcast(f32[8,128]{1,0:T(8,128)} %get-tuple-element.39), dimensions={1,2} | broadcast | bytes 69632 | tf_op jit(solution)/shard_map/broadcast_in_dim | solution.py:324
  66.0 12.6 %all-to-all-start = ((f32[16,8,128]{2,1,0:T(8,128)}), f32[16,8,128]{2,1,0:T(8,128)S(1)}, u32[]{:S(2)}, u32[]{:S(2)}) async-start(f32[16,8,128]{2,1,0:T(8,128)} %broadcast_in_dim.43), calls=%async_computation | async-start | bytes 131072 | tf_op jit(solution)/shard_map/all_to_all | solution.py:325
  79.9 6.3 %all-to-all-done = f32[16,8,128]{2,1,0:T(8,128)S(1)} async-done(((f32[16,8,128]{2,1,0:T(8,128)}), f32[16,8,128]{2,1,0:T(8,128)S(1)}, u32[]{:S(2)}, u32[]{:S(2)}) %all-to-all-start) | async-done | bytes 65568 | tf_op jit(solution)/shard_map/all_to_all | solution.py:325
  86.9 1.8 %fusion = (f32[]{:T(128)}, f32[4]{0:T(128)}) fusion(f32[]{:T(128)} %bitcast.21, f32[8]{0:T(128)S(1)} %reduce_sum.18), kind=kLoop, calls=%fused_computation.21 | loop fusion | flops 7 | bytes 40 | tf_op jit(solution)/shard_map/reduce_sum | solution.py:328
  (54 shorter events, 11.5 us)
Async XLA Ops:
  0.6 0.7 copy-start.13
  1.3 1.5 %copy-start.2 = (f32[8,1024]{1,0:T(8,128)S(1)}, f32[8,1024]{1,0:T(8,128)}, u32[]{:S(2)}) copy-start(f32[8,1024]{1,0:T(8,128)} %param.12) | copy-start | bytes 98308
  2.1 0.7 copy-start.15
  7.4 5.6 %copy-start.3 = (s32[6,1024]{1,0:T(8,128)S(1)}, s32[6,1024]{1,0:T(8,128)}, u32[]{:S(2)}) copy-start(s32[6,1024]{1,0:T(8,128)} %param.20) | copy-start | bytes 73732
  8.2 4.8 %copy-start = (f32[2,6,1024]{2,0,1:T(2,128)S(1)}, f32[2,6,1024]{2,0,1:T(2,128)}, u32[]{:S(2)}) copy-start(f32[2,6,1024]{2,0,1:T(2,128)} %param.14) | copy-start | bytes 147460
  8.2 7.5 %collective-permute-start = (f32[56,128]{1,0:T(8,128)S(1)}, f32[56,128]{1,0:T(8,128)S(1)}, u32[]{:S(2)}, u32[]{:S(2)}) collective-permute-start(f32[56,128]{1,0:T(8,128)S(1)} %get-tuple-element.51), channel_id=1, source_target_pairs={{0,2},{2,0},{4,6},{6,4},{8,10},{10,8},{12,14},{14,12},{16,18},{18,... | collective-permute-start | bytes 86024 | tf_op jit(solution)/shard_map/ppermute | solution.py:303
  11.0 4.7 %collective-permute-start.1 = (f32[56,128]{1,0:T(8,128)S(1)}, f32[56,128]{1,0:T(8,128)S(1)}, u32[]{:S(2)}, u32[]{:S(2)}) collective-permute-start(f32[56,128]{1,0:T(8,128)S(1)} %get-tuple-element.50), channel_id=1, source_target_pairs={{0,0},{2,4},{4,2},{6,8},{8,6},{10,12},{12,10},{14,16},{16,14},{18,... | collective-permute-start | bytes 86024 | tf_op jit(solution)/shard_map/ppermute | solution.py:303
  13.1 0.8 copy-start.4
  15.7 0.6 copy-start.6
  15.7 0.6 copy-start.8
  23.1 6.1 %collective-permute-start.2 = (f32[56,128]{1,0:T(8,128)S(1)}, f32[56,128]{1,0:T(8,128)S(1)}, u32[]{:S(2)}, u32[]{:S(2)}) collective-permute-start(f32[56,128]{1,0:T(8,128)S(1)} %get-tuple-element.49), channel_id=1, source_target_pairs={{0,2},{2,0},{4,6},{6,4},{8,10},{10,8},{12,14},{14,12},{16,18},{18,... | collective-permute-start | bytes 86024 | tf_op jit(solution)/shard_map/ppermute | solution.py:303
  27.3 1.9 %collective-permute-start.3 = (f32[56,128]{1,0:T(8,128)S(1)}, f32[56,128]{1,0:T(8,128)S(1)}, u32[]{:S(2)}, u32[]{:S(2)}) collective-permute-start(f32[56,128]{1,0:T(8,128)S(1)} %get-tuple-element.48), channel_id=1, source_target_pairs={{0,0},{2,4},{4,2},{6,8},{8,6},{10,12},{12,10},{14,16},{16,14},{18,... | collective-permute-start | bytes 86024 | tf_op jit(solution)/shard_map/ppermute | solution.py:303
  29.1 0.6 copy-start.9
  29.2 0.6 copy-start.11
  36.5 6.7 %collective-permute-start.4 = (f32[56,128]{1,0:T(8,128)S(1)}, f32[56,128]{1,0:T(8,128)S(1)}, u32[]{:S(2)}, u32[]{:S(2)}) collective-permute-start(f32[56,128]{1,0:T(8,128)S(1)} %get-tuple-element.47), channel_id=1, source_target_pairs={{0,2},{2,0},{4,6},{6,4},{8,10},{10,8},{12,14},{14,12},{16,18},{18,... | collective-permute-start | bytes 86024 | tf_op jit(solution)/shard_map/ppermute | solution.py:303
  41.4 1.9 %collective-permute-start.5 = (f32[56,128]{1,0:T(8,128)S(1)}, f32[56,128]{1,0:T(8,128)S(1)}, u32[]{:S(2)}, u32[]{:S(2)}) collective-permute-start(f32[56,128]{1,0:T(8,128)S(1)} %get-tuple-element.46), channel_id=1, source_target_pairs={{0,0},{2,4},{4,2},{6,8},{8,6},{10,12},{12,10},{14,16},{16,14},{18,... | collective-permute-start | bytes 86024 | tf_op jit(solution)/shard_map/ppermute | solution.py:303
  43.2 0.6 copy-start.10
  43.2 0.6 copy-start.12
  50.6 7.5 %collective-permute-start.6 = (f32[56,128]{1,0:T(8,128)S(1)}, f32[56,128]{1,0:T(8,128)S(1)}, u32[]{:S(2)}, u32[]{:S(2)}) collective-permute-start(f32[56,128]{1,0:T(8,128)S(1)} %get-tuple-element.45), channel_id=1, source_target_pairs={{0,2},{2,0},{4,6},{6,4},{8,10},{10,8},{12,14},{14,12},{16,18},{18,... | collective-permute-start | bytes 86024 | tf_op jit(solution)/shard_map/ppermute | solution.py:303
  56.3 1.9 %collective-permute-start.7 = (f32[56,128]{1,0:T(8,128)S(1)}, f32[56,128]{1,0:T(8,128)S(1)}, u32[]{:S(2)}, u32[]{:S(2)}) collective-permute-start(f32[56,128]{1,0:T(8,128)S(1)} %get-tuple-element.44), channel_id=1, source_target_pairs={{0,0},{2,4},{4,2},{6,8},{8,6},{10,12},{12,10},{14,16},{16,14},{18,... | collective-permute-start | bytes 86024 | tf_op jit(solution)/shard_map/ppermute | solution.py:303
  58.1 0.6 copy-start.7
  64.7 14.0 %copy-start.1 = (f32[48,1024]{1,0:T(8,128)S(1)}, f32[48,1024]{1,0:T(8,128)}, u32[]{:S(2)}) copy-start(f32[48,1024]{1,0:T(8,128)} %get-tuple-element.37) | copy-start | bytes 589828
  66.0 20.2 %all-to-all-start = ((f32[16,8,128]{2,1,0:T(8,128)}), f32[16,8,128]{2,1,0:T(8,128)S(1)}, u32[]{:S(2)}, u32[]{:S(2)}) async-start(f32[16,8,128]{2,1,0:T(8,128)} %broadcast_in_dim.43), calls=%async_computation | async-start | bytes 131072 | tf_op jit(solution)/shard_map/all_to_all | solution.py:325
  86.9 2.4 %copy-start.14 = (f32[1,1024]{1,0:T(1,128)S(1)}, f32[1,1024]{1,0:T(1,128)}, u32[]{:S(2)}) copy-start(f32[1,1024]{1,0:T(1,128)} %get-tuple-element.38) | copy-start | bytes 12292
  (1 other events, 0.6 us)

commit v2 on v1

--- a/solution.py
+++ b/solution.py
@@ -62,13 +62,16 @@
     return out
 
 
-def send_out(state, eta, send, outgoing):
+def send_out(even, state, eta, send, outgoing):
     rows, node_count = state.shape
     half = send.shape[1] // 2
     for side in range(2):
         for chunk in range(half // LANES):
-            first = side * half + chunk * LANES
-            ids = spread(send[0:1, first : first + LANES])
+            low = chunk * LANES
+            lower, upper = (send[0:1, i : i + LANES] for i in (low, half + low))
+            if side:
+                lower, upper = upper, lower
+            ids = spread(jnp.where(even, upper, lower))
             sources = []
             for number in range(node_count // LANES):
                 cols = slice(number * LANES, (number + 1) * LANES)
@@ -80,12 +83,29 @@
                 sources.append(own)
             found = pick(sources, ids & (LANES - 1), ids >> 7)
             for g, block in enumerate(found):
-                outgoing[
-                    side, g * SUBS : (g + 1) * SUBS, chunk * LANES : (chunk + 1) * LANES
-                ] = block
-
-
-def begin_kernel(parts, eta, bottom, node_area, send, state, outgoing, volume):
+                outgoing[side][g * SUBS : (g + 1) * SUBS, low : low + LANES] = block
+
+
+def prepare_kernel(flags, neighbours, grad_weights, lap_weights, near, weights):
+    near_count, node_count = neighbours.shape
+    half = (flags[3] - node_count) // 2
+    ids = neighbours[...]
+    first_ok, second_ok = (jnp.where(flags[i] > 0, 1.0, 0.0) for i in (1, 2))
+    own, low = ids < node_count, ids < node_count + half
+    swapped = jnp.where(own, ids, jnp.where(low, ids + half, ids - half))
+    ids = jnp.where(flags[0] > 0, swapped, ids)
+    valid = jnp.where(own, 1.0, jnp.where(ids < node_count + half, first_ok, second_ok))
+    near[...] = jnp.zeros(near.shape, jnp.int32)
+    weights[...] = jnp.zeros(weights.shape, jnp.float32)
+    near[:near_count, :] = ids
+    weights[0, :near_count, :] = grad_weights[0] * valid
+    weights[1, :near_count, :] = grad_weights[1] * valid
+    weights[2, :near_count, :] = lap_weights[...] * valid
+
+
+def begin_kernel(
+    flags, parts, eta, bottom, node_area, send, state, first_out, second_out, volume
+):
     shards, held, width = parts.shape
     fields, node_count = 3, eta.shape[1]
     level_count = shards * held
@@ -102,11 +122,11 @@
                 value = jnp.where(wet, value, 0.0)
             first = field * level_count + shard * held
             state[first : first + held, :] = value
-    send_out(state, eta, send, outgoing)
+    send_out(flags[0] > 0, state, eta, send, (first_out, second_out))
 
 
 def step_kernel(
-    edges,
+    flags,
     volume_in,
     state,
     eta,
@@ -119,20 +139,19 @@
     bottom,
     thickness,
     send,
-    new_state,
-    new_eta,
-    outgoing,
-    volume,
-    *,
+    *outputs,
     near_count,
     step,
 ):
+    last = step == STEPS - 1
+    if last:
+        velocity_out, density_out, new_eta, volume, new_state = outputs
+    else:
+        new_state, new_eta, first_out, second_out, volume = outputs
     rows, node_count = state.shape
     half = first_halo.shape[1]
     level_count = rows // 3
     groups = level_count // SUBS
-    slots = (node_count, node_count + half)
-    first_ok, second_ok = edges[0], edges[1]
 
     def source_blocks():
         for ref, width in ((state, node_count), (first_halo, half), (second_halo, half)):
@@ -156,8 +175,7 @@
         cols = pl.ds(pl.multiple_of(number * LANES, LANES), LANES)
         ids = neighbours[:, cols]
         lanes, blocks = ids & (LANES - 1), ids >> 7
-        valid = jnp.where(ids < slots[0], 1.0, jnp.where(ids < slots[1], first_ok, second_ok))
-        east, north, smooth = (weights[i, :, cols] * valid for i in range(3))
+        east, north, smooth = (weights[i, :, cols] for i in range(3))
         eta_here = eta[0:1, cols]
         (eta_near,) = pick(eta_sources, lanes, blocks)
         eta_differ = eta_near - spread(eta_here)
@@ -228,11 +246,29 @@
         0, node_count // LANES, tile, jnp.zeros((1, LANES), jnp.float32)
     )
     volume[...] = jnp.where(sub == step, spread(total), volume_in[...])
-    send_out(new_state, new_eta, send, outgoing)
+    if last:
+        held = density_out.shape[0]
+        for field in range(3):
+            first = pl.multiple_of(field * level_count + flags[4] * held, SUBS)
+            value = new_state[pl.ds(first, held), :]
+            if field < 2:
+                velocity_out[field] = value
+            else:
+                density_out[...] = value
+    else:
+        send_out(flags[0] > 0, new_state, new_eta, send, (first_out, second_out))
 
 
 def vmem(count):
     return [pl.BlockSpec(memory_space=pltpu.VMEM)] * count
+
+
+def kept(*dims, dtype=jnp.float32):
+    return pltpu.VMEM(dims, dtype)
+
+
+def keep(array):
+    return pltpu.with_memory_space_constraint(array, pltpu.VMEM)
 
 
 def shape(*dims):
@@ -271,64 +307,101 @@
             )
         ]
         even = space_rank % 2 == 0
-        send = jnp.where(even, jnp.roll(send_list, half, axis=1), send_list)
-        swapped = neighbours + jnp.where(neighbours < node_count + half, half, -half)
-        near = jnp.where(even & (neighbours >= node_count), swapped, neighbours)
         low, high = space_rank > 0, space_rank < ends
-        edges = jnp.stack([jnp.where(even, high, low), jnp.where(even, low, high)])
-        edges = edges.astype(jnp.float32)
+        flags = jnp.stack(
+            [
+                even.astype(jnp.int32),
+                jnp.where(even, high, low).astype(jnp.int32),
+                jnp.where(even, low, high).astype(jnp.int32),
+                jnp.int32(node_count + 2 * half),
+                level_rank.astype(jnp.int32),
+            ]
+        )
 
         thick = jnp.broadcast_to(thickness[:, None], (held, LANES))
         own = jnp.concatenate([velocity[0], velocity[1], density, thick], axis=1)
         parts = lax.all_gather(own, "level")
         thick = parts[:, :, 3 * node_count :].reshape(level_count, LANES)
         pad = -near_count % SUBS
-        near = jnp.pad(near, ((0, pad), (0, 0)))
-        weights = jnp.concatenate([grad_weights, lap_weights[None]], axis=0)
-        weights = jnp.pad(weights, ((0, 0), (0, pad), (0, 0)))
+        near_rows = near_count + pad
         eta = elevation[None]
         depth = bottom[None]
         area = node_area[None]
-        out_shape = shape(2, rows + SUBS, half)
-
-        state, outgoing, volume = pl.pallas_call(
+        scalars = [pl.BlockSpec(memory_space=pltpu.SMEM)]
+        halo = (rows + SUBS, half)
+
+        state, *outgoing, volume = pl.pallas_call(
             begin_kernel,
-            out_shape=(shape(rows, node_count), out_shape, shape(SUBS, LANES)),
-            in_specs=vmem(5),
-            out_specs=tuple(vmem(3)),
+            out_shape=(kept(rows, node_count), kept(*halo), kept(*halo), kept(SUBS, LANES)),
+            in_specs=scalars + vmem(5),
+            out_specs=tuple(vmem(4)),
             name="begin",
-        )(parts, eta, depth, area, send)
+        )(flags, parts, eta, depth, area, send_list)
+        near, weights = pl.pallas_call(
+            prepare_kernel,
+            out_shape=(
+                kept(near_rows, node_count, dtype=jnp.int32),
+                kept(3, near_rows, node_count),
+            ),
+            in_specs=scalars + vmem(3),
+            out_specs=tuple(vmem(2)),
+            name="prepare",
+        )(flags, neighbours, grad_weights, lap_weights)
+        fixed = (near, weights, coriolis[None], area, depth, thick, send_list)
+        fixed = tuple(map(keep, fixed))
 
         for step in range(STEPS):
-            halos = [lax.ppermute(outgoing[i], "space", rounds[i]) for i in range(2)]
+            halos = [
+                keep(lax.ppermute(value, "space", pairs))
+                for value, pairs in zip(outgoing, rounds)
+            ]
 
             def body(*refs, step=step):
                 step_kernel(*refs, near_count=near_count, step=step)
 
-            state, eta, outgoing, volume = pl.pallas_call(
+            last = step == STEPS - 1
+            if last:
+                outs = (
+                    shape(2, held, node_count),
+                    shape(held, node_count),
+                    kept(1, node_count),
+                    kept(SUBS, LANES),
+                )
+                scratch = [pltpu.VMEM((rows, node_count), jnp.float32)]
+            else:
+                outs = (
+                    kept(rows, node_count),
+                    kept(1, node_count),
+                    kept(*halo),
+                    kept(*halo),
+                    kept(SUBS, LANES),
+                )
+                scratch = []
+            results = pl.pallas_call(
                 body,
-                out_shape=(
-                    shape(rows, node_count),
-                    shape(1, node_count),
-                    out_shape,
-                    shape(SUBS, LANES),
-                ),
-                in_specs=[pl.BlockSpec(memory_space=pltpu.SMEM)] + vmem(12),
-                out_specs=tuple(vmem(4)),
+                out_shape=outs,
+                in_specs=scalars + vmem(12),
+                out_specs=tuple(vmem(len(outs))),
+                scratch_shapes=scratch,
                 name="step",
-            )(
-                edges, volume, state, eta, *halos, near, weights,
-                coriolis[None], area, depth, thick, send,
-            )
-
-        shared = jnp.broadcast_to(volume, (space_count,) + volume.shape)
-        shared = lax.all_to_all(shared, "space", 0, 0)
-        summed = jnp.sum(shared, axis=(0, 2))
+            )(flags, *map(keep, (volume, state, eta)), *halos, *fixed)
+            if last:
+                velocity_out, density_out, eta, volume = results
+            else:
+                state, eta, *outgoing, volume = results
+
+        if space_count & (space_count - 1):
+            volume = lax.psum(volume, "space")
+        else:
+            distance = 1
+            while distance < space_count:
+                pairs = [(i, i ^ distance) for i in range(space_count)]
+                volume = volume + lax.ppermute(volume, "space", pairs)
+                distance *= 2
+        summed = jnp.sum(volume, axis=1)
         drifts = summed[:STEPS] / summed[STEPS]
         eta = eta[0] + time_step * jnp.sum(drifts)
-        fields = state.reshape(3, level_count, node_count)
-        mine = lax.dynamic_slice_in_dim(fields, level_rank * held, held, axis=1)
-        return mine[:2], mine[2], eta, drifts
+        return velocity_out, density_out, eta, drifts
 
     return local
 

time: 90.9 us -> 80.1 us (0.88)
  local copies, waits for them, and re-layouts: 13.6 us -> 4.09 us
  starting transfers between devices: 32.9 us -> 37.2 us
  Pallas kernels: 25.6 us -> 22.2 us
  other arithmetic: 4.35 us -> 2.52 us
    ppermute x8 -> x12, starting transfers between devices: 20.2 us -> 37.2 us  [the longest x8 22 us: local(): lax.ppermute(value, 'space', pairs)]
    all_to_all x1 -> x0, starting transfers between devices: 12.6 us -> none  [local(): shared = lax.all_to_all(shared, 'space', 0, 0)]
    ppermute x8 -> x12, waiting for transfers between devices: 3.57 us -> 9.92 us  [the longest x4 6.34 us: local(): volume = volume + lax.ppermute(volume, 'space', pairs)]
    all_to_all x1 -> x0, waiting for transfers between devices: 6.26 us -> none  [local(): shared = lax.all_to_all(shared, 'space', 0, 0)]
    squeeze x5 -> x0, local copies, waits for them, and re-layouts: 3.71 us -> none  [the longest x4 3.08 us: local(): halos = [lax.ppermute(outgoing[i], 'space', rounds[i]) for i in range(2)]]
    pallas_call x5 -> x6, Pallas kernels: 25.6 us -> 22.2 us  [the longest x4 20.1 us: local(): pl.pallas_call(body, out_shape=outs, in_specs=scalars + vmem(12), out_spe...]
    unnamed x33 -> x17, local copies, waits for them, and re-layouts: 4.53 us -> 1.33 us
    broadcast_in_dim x1 -> x0, local copies, waits for them, and re-layouts: 1.36 us -> none  [local(): shared = jnp.broadcast_to(volume, (space_count,) + volume.shape)]
  transfers between devices with their start and end apart: 9 -> 12, of which waited for: 4 -> 7; matrix products, arithmetic and copies ran while one was open for 5% -> 2% of each run, Pallas kernels for 0% -> 1%
where the time goes in v2:
time: 80.1 us; the launch traced here: 79.6 us
  starting transfers between devices  37.2 us (46%)
  Pallas kernels  22.2 us (28%)
  waiting for transfers between devices  9.92 us (12%)
  local copies, waits for them, and re-layouts  4.09 us (5%)
  other arithmetic  2.52 us (3%)
  blocking collectives  2.22 us (3%)
  between operations  1.46 us (2%)
    ppermute x8, starting transfers between devices, local(): lax.ppermute(value, 'space', pairs)  22 us
    pallas_call x4, Pallas kernels, local(): pl.pallas_call(body, out_shape=outs, in_specs=scalars + vmem(12), out_spe...  20.1 us
    ppermute x4, starting transfers between devices, local(): volume = volume + lax.ppermute(volume, 'space', pairs)  15.2 us
    ppermute x4, waiting for transfers between devices, local(): volume = volume + lax.ppermute(volume, 'space', pairs)  6.34 us
    ppermute x8, waiting for transfers between devices, local(): lax.ppermute(value, 'space', pairs)  3.59 us
    all_gather x1, blocking collectives, local(): parts = lax.all_gather(own, 'level')  2.22 us
    reduce_sum x1, other arithmetic, local(): eta = eta[0] + time_step * jnp.sum(drifts)  1.79 us
  transfers between devices with their start and end apart: 12, of which 7 were waited for; matrix products, arithmetic and copies ran while one was open for 2% of the time, Pallas kernels for 1%

profile of v2, /device:TPU:0, one launch (start us, length us, event | category | flops | bytes accessed | tf_op | source)
XLA Modules:
  0.0 79.6 jit_solution(2010642253024008015)
XLA Ops:
  0.7 0.8 slice_bitcast_fusion.1
  1.6 2.2 %all-gather = f32[16,3200]{1,0:T(8,128)} all-gather(f32[8,3200]{1,0:T(8,128)S(1)} %pad_maximum_fusion), channel_id=2, replica_groups=mesh['space'=16,'level'=2] {'level'}, dimensions={0}, use_global_device_ids=true | all-gather | bytes 307200 | tf_op jit(solution)/shard_map/all_gather | solution.py:323
  4.4 1.2 %begin.1 = (f32[48,1024]{1,0:T(8,128)S(1)}, f32[56,128]{1,0:T(8,128)S(1)}, f32[56,128]{1,0:T(8,128)S(1)}, f32[8,128]{1,0:T(8,128)S(1)}) custom-call(s32[5]{0:T(128)} %stack.31.flags.refs_0_, f32[2,8,3200]{2,1,0:T(8,128)} %bitcast.33, f32[1,1024]{1,0:T(1,128)} %bitcast.31, s32[1,1024]{1,0:T(1,128)} %bitcast.17, f32[1,1024]{1,0:T(1,128)} %bitcast.22, ...), custom_call_target="tpu_custom_call" | custom-call | tf_op jit(solution)/shard_map/begin/pallas_call | solution.py:333
  5.5 2.9 %collective-permute-start = (f32[56,128]{1,0:T(8,128)S(1)}, f32[56,128]{1,0:T(8,128)S(1)}, u32[]{:S(2)}, u32[]{:S(2)}) collective-permute-start(f32[56,128]{1,0:T(8,128)S(1)} %get-tuple-element.31), channel_id=1, source_target_pairs={{0,2},{2,0},{4,6},{6,4},{8,10},{10,8},{12,14},{14,12},{16,18},{18,... | collective-permute-start | bytes 86024 | tf_op jit(solution)/shard_map/ppermute | solution.py:355
  10.5 0.9 %prepare.1 = (s32[8,1024]{1,0:T(8,128)S(1)}, f32[3,8,1024]{2,1,0:T(8,128)S(1)}) custom-call(s32[5]{0:T(128)} %stack.31.flags.refs_0_, s32[6,1024]{1,0:T(8,128)} %neighbours.1, f32[2,6,1024]{2,1,0:T(8,128)} %copy.15.grad_weights, f32[6,1024]{1,0:T(8,128)} %lap_weights.1), custom_call_target="tpu_custom_call" | custom-call | tf_op jit(solution)/shard_map/prepare/pallas_call | solution.py:340
  12.1 4.9 %step.4 = (f32[48,1024]{1,0:T(8,128)S(1)}, f32[1,1024]{1,0:T(1,128)S(1)}, f32[56,128]{1,0:T(8,128)S(1)}, f32[56,128]{1,0:T(8,128)S(1)}, f32[8,128]{1,0:T(8,128)S(1)}) custom-call(s32[5]{0:T(128)} %stack.31.flags.refs_0_, f32[8,128]{1,0:T(8,128)S(1)} %get-tuple-element.29.refs_1_, f32[48,1024]{1,0:T(8,128)S(1)} %get-tuple-element.30.refs_2_, ...), custom_call_target="tpu_custom_call" | custom-call | tf_op jit(solution)/shard_map/step/pallas_call | solution.py:380
  17.0 4.3 %collective-permute-start.2 = (f32[56,128]{1,0:T(8,128)S(1)}, f32[56,128]{1,0:T(8,128)S(1)}, u32[]{:S(2)}, u32[]{:S(2)}) collective-permute-start(f32[56,128]{1,0:T(8,128)S(1)} %get-tuple-element.38), channel_id=1, source_target_pairs={{0,2},{2,0},{4,6},{6,4},{8,10},{10,8},{12,14},{14,12},{16,18},{18,... | collective-permute-start | bytes 86024 | tf_op jit(solution)/shard_map/ppermute | solution.py:355
  22.0 1.2 %collective-permute-done.2.refs_4_ = f32[56,128]{1,0:T(8,128)S(1)} collective-permute-done((f32[56,128]{1,0:T(8,128)S(1)}, f32[56,128]{1,0:T(8,128)S(1)}, u32[]{:S(2)}, u32[]{:S(2)}) %collective-permute-start.2) | collective-permute-done | bytes 28704 | tf_op jit(solution)/shard_map/ppermute | solution.py:355
  23.2 4.9 %step.5 = (f32[48,1024]{1,0:T(8,128)S(1)}, f32[1,1024]{1,0:T(1,128)S(1)}, f32[56,128]{1,0:T(8,128)S(1)}, f32[56,128]{1,0:T(8,128)S(1)}, f32[8,128]{1,0:T(8,128)S(1)}) custom-call(s32[5]{0:T(128)} %stack.31.flags.refs_0_, f32[8,128]{1,0:T(8,128)S(1)} %get-tuple-element.35.refs_1_, f32[48,1024]{1,0:T(8,128)S(1)} %get-tuple-element.36.refs_2_, ...), custom_call_target="tpu_custom_call" | custom-call | tf_op jit(solution)/shard_map/step/pallas_call | solution.py:380
  28.1 5.8 %collective-permute-start.4 = (f32[56,128]{1,0:T(8,128)S(1)}, f32[56,128]{1,0:T(8,128)S(1)}, u32[]{:S(2)}, u32[]{:S(2)}) collective-permute-start(f32[56,128]{1,0:T(8,128)S(1)} %get-tuple-element.43), channel_id=1, source_target_pairs={{0,2},{2,0},{4,6},{6,4},{8,10},{10,8},{12,14},{14,12},{16,18},{18,... | collective-permute-start | bytes 86024 | tf_op jit(solution)/shard_map/ppermute | solution.py:355
  34.6 1.2 %collective-permute-done.4.refs_4_ = f32[56,128]{1,0:T(8,128)S(1)} collective-permute-done((f32[56,128]{1,0:T(8,128)S(1)}, f32[56,128]{1,0:T(8,128)S(1)}, u32[]{:S(2)}, u32[]{:S(2)}) %collective-permute-start.4) | collective-permute-done | bytes 28704 | tf_op jit(solution)/shard_map/ppermute | solution.py:355
  35.8 5.0 %step.6 = (f32[48,1024]{1,0:T(8,128)S(1)}, f32[1,1024]{1,0:T(1,128)S(1)}, f32[56,128]{1,0:T(8,128)S(1)}, f32[56,128]{1,0:T(8,128)S(1)}, f32[8,128]{1,0:T(8,128)S(1)}) custom-call(s32[5]{0:T(128)} %stack.31.flags.refs_0_, f32[8,128]{1,0:T(8,128)S(1)} %get-tuple-element.40.refs_1_, f32[48,1024]{1,0:T(8,128)S(1)} %get-tuple-element.41.refs_2_, ...), custom_call_target="tpu_custom_call" | custom-call | tf_op jit(solution)/shard_map/step/pallas_call | solution.py:380
  40.8 6.4 %collective-permute-start.6 = (f32[56,128]{1,0:T(8,128)S(1)}, f32[56,128]{1,0:T(8,128)S(1)}, u32[]{:S(2)}, u32[]{:S(2)}) collective-permute-start(f32[56,128]{1,0:T(8,128)S(1)} %get-tuple-element.48), channel_id=1, source_target_pairs={{0,2},{2,0},{4,6},{6,4},{8,10},{10,8},{12,14},{14,12},{16,18},{18,... | collective-permute-start | bytes 86024 | tf_op jit(solution)/shard_map/ppermute | solution.py:355
  47.8 1.2 %collective-permute-done.6.refs_4_ = f32[56,128]{1,0:T(8,128)S(1)} collective-permute-done((f32[56,128]{1,0:T(8,128)S(1)}, f32[56,128]{1,0:T(8,128)S(1)}, u32[]{:S(2)}, u32[]{:S(2)}) %collective-permute-start.6) | collective-permute-done | bytes 28704 | tf_op jit(solution)/shard_map/ppermute | solution.py:355
  49.0 5.4 %step.7 = (f32[2,8,1024]{2,1,0:T(8,128)}, f32[8,1024]{1,0:T(8,128)}, f32[1,1024]{1,0:T(1,128)S(1)}, f32[8,128]{1,0:T(8,128)S(1)}) custom-call(s32[5]{0:T(128)} %stack.31.flags.refs_0_, f32[8,128]{1,0:T(8,128)S(1)} %get-tuple-element.45.refs_1_, f32[48,1024]{1,0:T(8,128)S(1)} %get-tuple-element.46.refs_2_, f32[1,1024]{1,0:T(1,128)S(1)} %get-tuple-element.47.refs_3_, ...), custom_call_target="tpu_custom_call" | custom-call | tf_op jit(solution)/shard_map/step/pallas_call | solution.py:380
  54.3 6.2 %collective-permute-start.8 = (f32[8,128]{1,0:T(8,128)S(1)}, f32[8,128]{1,0:T(8,128)S(1)}, u32[]{:S(2)}, u32[]{:S(2)}) collective-permute-start(f32[8,128]{1,0:T(8,128)S(1)} %get-tuple-element.53), channel_id=1, source_target_pairs={{0,2},{2,0},{4,6},{6,4},{8,10},{10,8},{12,14},{14,12},{16,18},{18,... | collective-permute-start | bytes 12296 | tf_op jit(solution)/shard_map/ppermute | solution.py:399
  60.6 1.6 %collective-permute-done.8 = f32[8,128]{1,0:T(8,128)S(1)} collective-permute-done((f32[8,128]{1,0:T(8,128)S(1)}, f32[8,128]{1,0:T(8,128)S(1)}, u32[]{:S(2)}, u32[]{:S(2)}) %collective-permute-start.8) | collective-permute-done | bytes 4128 | tf_op jit(solution)/shard_map/ppermute | solution.py:399
  62.1 3.5 %collective-permute-start.9 = (f32[8,128]{1,0:T(8,128)S(1)}, f32[8,128]{1,0:T(8,128)S(1)}, u32[]{:S(2)}, u32[]{:S(2)}) collective-permute-start(f32[8,128]{1,0:T(8,128)S(1)} %add.26), channel_id=1, source_target_pairs={{0,4},{2,6},{4,0},{6,2},{8,12},{10,14},{12,8},{14,10},{16,20},{18,... | collective-permute-start | bytes 12296 | tf_op jit(solution)/shard_map/ppermute | solution.py:399
  65.6 1.6 %collective-permute-done.9 = f32[8,128]{1,0:T(8,128)S(1)} collective-permute-done((f32[8,128]{1,0:T(8,128)S(1)}, f32[8,128]{1,0:T(8,128)S(1)}, u32[]{:S(2)}, u32[]{:S(2)}) %collective-permute-start.9) | collective-permute-done | bytes 4128 | tf_op jit(solution)/shard_map/ppermute | solution.py:399
  67.2 2.5 %collective-permute-start.10 = (f32[8,128]{1,0:T(8,128)S(1)}, f32[8,128]{1,0:T(8,128)S(1)}, u32[]{:S(2)}, u32[]{:S(2)}) collective-permute-start(f32[8,128]{1,0:T(8,128)S(1)} %add.27), channel_id=1, source_target_pairs={{0,8},{2,10},{4,12},{6,14},{8,0},{10,2},{12,4},{14,6},{16,24},{18,... | collective-permute-start | bytes 12296 | tf_op jit(solution)/shard_map/ppermute | solution.py:399
  69.7 1.6 %collective-permute-done.10 = f32[8,128]{1,0:T(8,128)S(1)} collective-permute-done((f32[8,128]{1,0:T(8,128)S(1)}, f32[8,128]{1,0:T(8,128)S(1)}, u32[]{:S(2)}, u32[]{:S(2)}) %collective-permute-start.10) | collective-permute-done | bytes 4128 | tf_op jit(solution)/shard_map/ppermute | solution.py:399
  71.3 3.0 %collective-permute-start.11 = (f32[8,128]{1,0:T(8,128)S(1)}, f32[8,128]{1,0:T(8,128)S(1)}, u32[]{:S(2)}, u32[]{:S(2)}) collective-permute-start(f32[8,128]{1,0:T(8,128)S(1)} %add.28), channel_id=1, source_target_pairs={{0,16},{2,18},{4,20},{6,22},{8,24},{10,26},{12,28},{14,30},{16,0},... | collective-permute-start | bytes 12296 | tf_op jit(solution)/shard_map/ppermute | solution.py:399
  74.3 1.6 %collective-permute-done.11 = f32[8,128]{1,0:T(8,128)S(1)} collective-permute-done((f32[8,128]{1,0:T(8,128)S(1)}, f32[8,128]{1,0:T(8,128)S(1)}, u32[]{:S(2)}, u32[]{:S(2)}) %collective-permute-start.11) | collective-permute-done | bytes 4128 | tf_op jit(solution)/shard_map/ppermute | solution.py:399
  76.6 1.8 %fusion = (f32[]{:T(128)}, f32[4]{0:T(128)}) fusion(f32[]{:T(128)} %bitcast.12, f32[8]{0:T(128)S(1)} %add_reduce_fusion), kind=kLoop, calls=%fused_computation.7 | loop fusion | flops 7 | bytes 40 | tf_op jit(solution)/shard_map/reduce_sum | solution.py:403
  (36 shorter events, 6.6 us)
Async XLA Ops:
  0.7 0.8 %copy-start.7 = (f32[8]{0:T(128)S(1)}, f32[8]{0:T(128)}, u32[]{:S(2)}) copy-start(f32[8]{0:T(128)} %param.18) | copy-start | bytes 100
  0.7 0.9 %copy-start.6 = (f32[8,1024]{1,0:T(8,128)S(1)}, f32[8,1024]{1,0:T(8,128)}, u32[]{:S(2)}) copy-start(f32[8,1024]{1,0:T(8,128)} %param.12) | copy-start | bytes 98308
  4.4 5.5 %copy-start.5 = (f32[2,6,1024]{2,0,1:T(2,128)S(1)}, f32[2,6,1024]{2,0,1:T(2,128)}, u32[]{:S(2)}) copy-start(f32[2,6,1024]{2,0,1:T(2,128)} %param.14) | copy-start | bytes 147460
  5.5 5.8 %collective-permute-start = (f32[56,128]{1,0:T(8,128)S(1)}, f32[56,128]{1,0:T(8,128)S(1)}, u32[]{:S(2)}, u32[]{:S(2)}) collective-permute-start(f32[56,128]{1,0:T(8,128)S(1)} %get-tuple-element.31), channel_id=1, source_target_pairs={{0,2},{2,0},{4,6},{6,4},{8,10},{10,8},{12,14},{14,12},{16,18},{18,... | collective-permute-start | bytes 86024 | tf_op jit(solution)/shard_map/ppermute | solution.py:355
  8.4 3.0 %collective-permute-start.1 = (f32[56,128]{1,0:T(8,128)S(1)}, f32[56,128]{1,0:T(8,128)S(1)}, u32[]{:S(2)}, u32[]{:S(2)}) collective-permute-start(f32[56,128]{1,0:T(8,128)S(1)} %get-tuple-element.32), channel_id=1, source_target_pairs={{0,0},{2,4},{4,2},{6,8},{8,6},{10,12},{12,10},{14,16},{16,14},{18,... | collective-permute-start | bytes 86024 | tf_op jit(solution)/shard_map/ppermute | solution.py:355
  10.5 1.0 %copy-start.2 = (f32[1024]{0:T(1024)S(1)}, f32[1024]{0:T(1024)}, u32[]{:S(2)}) copy-start(f32[1024]{0:T(1024)} %param.16) | copy-start | bytes 12292
  10.5 1.0 %copy-start.4 = (f32[1024]{0:T(1024)S(1)}, f32[1024]{0:T(1024)}, u32[]{:S(2)}) copy-start(f32[1024]{0:T(1024)} %param.13) | copy-start | bytes 12292
  11.4 0.7 copy-start.1
  11.4 0.7 copy-start
  11.4 0.7 copy-start.3
  17.0 6.1 %collective-permute-start.2 = (f32[56,128]{1,0:T(8,128)S(1)}, f32[56,128]{1,0:T(8,128)S(1)}, u32[]{:S(2)}, u32[]{:S(2)}) collective-permute-start(f32[56,128]{1,0:T(8,128)S(1)} %get-tuple-element.38), channel_id=1, source_target_pairs={{0,2},{2,0},{4,6},{6,4},{8,10},{10,8},{12,14},{14,12},{16,18},{18,... | collective-permute-start | bytes 86024 | tf_op jit(solution)/shard_map/ppermute | solution.py:355
  21.3 1.9 %collective-permute-start.3 = (f32[56,128]{1,0:T(8,128)S(1)}, f32[56,128]{1,0:T(8,128)S(1)}, u32[]{:S(2)}, u32[]{:S(2)}) collective-permute-start(f32[56,128]{1,0:T(8,128)S(1)} %get-tuple-element.39), channel_id=1, source_target_pairs={{0,0},{2,4},{4,2},{6,8},{8,6},{10,12},{12,10},{14,16},{16,14},{18,... | collective-permute-start | bytes 86024 | tf_op jit(solution)/shard_map/ppermute | solution.py:355
  28.1 7.7 %collective-permute-start.4 = (f32[56,128]{1,0:T(8,128)S(1)}, f32[56,128]{1,0:T(8,128)S(1)}, u32[]{:S(2)}, u32[]{:S(2)}) collective-permute-start(f32[56,128]{1,0:T(8,128)S(1)} %get-tuple-element.43), channel_id=1, source_target_pairs={{0,2},{2,0},{4,6},{6,4},{8,10},{10,8},{12,14},{14,12},{16,18},{18,... | collective-permute-start | bytes 86024 | tf_op jit(solution)/shard_map/ppermute | solution.py:355
  33.9 1.9 %collective-permute-start.5 = (f32[56,128]{1,0:T(8,128)S(1)}, f32[56,128]{1,0:T(8,128)S(1)}, u32[]{:S(2)}, u32[]{:S(2)}) collective-permute-start(f32[56,128]{1,0:T(8,128)S(1)} %get-tuple-element.44), channel_id=1, source_target_pairs={{0,0},{2,4},{4,2},{6,8},{8,6},{10,12},{12,10},{14,16},{16,14},{18,... | collective-permute-start | bytes 86024 | tf_op jit(solution)/shard_map/ppermute | solution.py:355
  40.8 8.2 %collective-permute-start.6 = (f32[56,128]{1,0:T(8,128)S(1)}, f32[56,128]{1,0:T(8,128)S(1)}, u32[]{:S(2)}, u32[]{:S(2)}) collective-permute-start(f32[56,128]{1,0:T(8,128)S(1)} %get-tuple-element.48), channel_id=1, source_target_pairs={{0,2},{2,0},{4,6},{6,4},{8,10},{10,8},{12,14},{14,12},{16,18},{18,... | collective-permute-start | bytes 86024 | tf_op jit(solution)/shard_map/ppermute | solution.py:355
  47.1 1.9 %collective-permute-start.7 = (f32[56,128]{1,0:T(8,128)S(1)}, f32[56,128]{1,0:T(8,128)S(1)}, u32[]{:S(2)}, u32[]{:S(2)}) collective-permute-start(f32[56,128]{1,0:T(8,128)S(1)} %get-tuple-element.49), channel_id=1, source_target_pairs={{0,0},{2,4},{4,2},{6,8},{8,6},{10,12},{12,10},{14,16},{16,14},{18,... | collective-permute-start | bytes 86024 | tf_op jit(solution)/shard_map/ppermute | solution.py:355
  54.3 7.8 %collective-permute-start.8 = (f32[8,128]{1,0:T(8,128)S(1)}, f32[8,128]{1,0:T(8,128)S(1)}, u32[]{:S(2)}, u32[]{:S(2)}) collective-permute-start(f32[8,128]{1,0:T(8,128)S(1)} %get-tuple-element.53), channel_id=1, source_target_pairs={{0,2},{2,0},{4,6},{6,4},{8,10},{10,8},{12,14},{14,12},{16,18},{18,... | collective-permute-start | bytes 12296 | tf_op jit(solution)/shard_map/ppermute | solution.py:399
  62.1 5.1 %collective-permute-start.9 = (f32[8,128]{1,0:T(8,128)S(1)}, f32[8,128]{1,0:T(8,128)S(1)}, u32[]{:S(2)}, u32[]{:S(2)}) collective-permute-start(f32[8,128]{1,0:T(8,128)S(1)} %add.26), channel_id=1, source_target_pairs={{0,4},{2,6},{4,0},{6,2},{8,12},{10,14},{12,8},{14,10},{16,20},{18,... | collective-permute-start | bytes 12296 | tf_op jit(solution)/shard_map/ppermute | solution.py:399
  67.2 4.1 %collective-permute-start.10 = (f32[8,128]{1,0:T(8,128)S(1)}, f32[8,128]{1,0:T(8,128)S(1)}, u32[]{:S(2)}, u32[]{:S(2)}) collective-permute-start(f32[8,128]{1,0:T(8,128)S(1)} %add.27), channel_id=1, source_target_pairs={{0,8},{2,10},{4,12},{6,14},{8,0},{10,2},{12,4},{14,6},{16,24},{18,... | collective-permute-start | bytes 12296 | tf_op jit(solution)/shard_map/ppermute | solution.py:399
  71.3 4.6 %collective-permute-start.11 = (f32[8,128]{1,0:T(8,128)S(1)}, f32[8,128]{1,0:T(8,128)S(1)}, u32[]{:S(2)}, u32[]{:S(2)}) collective-permute-start(f32[8,128]{1,0:T(8,128)S(1)} %add.28), channel_id=1, source_target_pairs={{0,16},{2,18},{4,20},{6,22},{8,24},{10,26},{12,28},{14,30},{16,0},... | collective-permute-start | bytes 12296 | tf_op jit(solution)/shard_map/ppermute | solution.py:399

commit v3 on v2

--- a/solution.py
+++ b/solution.py
@@ -257,6 +257,13 @@
                 density_out[...] = value
     else:
         send_out(flags[0] > 0, new_state, new_eta, send, (first_out, second_out))
+
+
+def finish_kernel(volume, eta, eta_out, drifts):
+    summed = jnp.sum(volume[...], axis=1, keepdims=True)
+    ratio = summed / summed[STEPS : STEPS + 1, :]
+    eta_out[...] = eta[...] + time_step * jnp.sum(ratio[:STEPS], axis=0, keepdims=True)
+    drifts[...] = jnp.broadcast_to(ratio, drifts.shape)
 
 
 def vmem(count):
@@ -398,10 +405,14 @@
                 pairs = [(i, i ^ distance) for i in range(space_count)]
                 volume = volume + lax.ppermute(volume, "space", pairs)
                 distance *= 2
-        summed = jnp.sum(volume, axis=1)
-        drifts = summed[:STEPS] / summed[STEPS]
-        eta = eta[0] + time_step * jnp.sum(drifts)
-        return velocity_out, density_out, eta, drifts
+        eta, drifts = pl.pallas_call(
+            finish_kernel,
+            out_shape=(shape(1, node_count), shape(SUBS, LANES)),
+            in_specs=vmem(2),
+            out_specs=tuple(vmem(2)),
+            name="finish",
+        )(keep(volume), keep(eta))
+        return velocity_out, density_out, eta[0], drifts[:STEPS, 0]
 
     return local
 

time: 80.1 us -> 78.4 us (0.979)
  other arithmetic: 2.52 us -> 0.02 us
    reduce_sum x2 -> x0, other arithmetic: 1.91 us -> none  [the longest x1 1.79 us: local(): eta = eta[0] + time_step * jnp.sum(drifts)]
where the time goes in v3:
time: 78.4 us; the launch traced here: 77.9 us
  starting transfers between devices  37.2 us (47%)
  Pallas kernels  22.9 us (29%)
  waiting for transfers between devices  9.92 us (13%)
  local copies, waits for them, and re-layouts  4.79 us (6%)
  blocking collectives  2.22 us (3%)
  between operations  0.82 us (1%)
    ppermute x8, starting transfers between devices, local(): lax.ppermute(value, 'space', pairs)  22 us
    pallas_call x4, Pallas kernels, local(): pl.pallas_call(body, out_shape=outs, in_specs=scalars + vmem(12), out_spe...  20.1 us
    ppermute x4, starting transfers between devices, local(): volume = volume + lax.ppermute(volume, 'space', pairs)  15.2 us
    ppermute x4, waiting for transfers between devices, local(): volume = volume + lax.ppermute(volume, 'space', pairs)  6.34 us
    ppermute x8, waiting for transfers between devices, local(): lax.ppermute(value, 'space', pairs)  3.59 us
    all_gather x1, blocking collectives, local(): parts = lax.all_gather(own, 'level')  2.22 us
  transfers between devices with their start and end apart: 12, of which 7 were waited for; matrix products, arithmetic and copies ran while one was open for 2% of the time, Pallas kernels for 1%

profile of v3, /device:TPU:0, one launch (start us, length us, event | category | flops | bytes accessed | tf_op | source)
XLA Modules:
  0.0 77.9 jit_solution(14150046993817163830)
XLA Ops:
  0.7 0.8 %slice_bitcast_fusion.1 = (f32[8,1024]{1,0:T(8,128)S(1)}, f32[8,1024]{1,0:T(8,128)S(1)}) fusion(f32[2,8,1024]{2,1,0:T(8,128)} %param.11), kind=kLoop, calls=%fused_computation.2 | loop fusion | bytes 131072 | tf_op jit(solution)/shard_map/squeeze | solution.py:329
  1.6 2.2 %all-gather = f32[16,3200]{1,0:T(8,128)} all-gather(f32[8,3200]{1,0:T(8,128)S(1)} %pad_maximum_fusion), channel_id=2, replica_groups=mesh['space'=16,'level'=2] {'level'}, dimensions={0}, use_global_device_ids=true | all-gather | bytes 307200 | tf_op jit(solution)/shard_map/all_gather | solution.py:330
  4.4 1.2 %begin.1 = (f32[48,1024]{1,0:T(8,128)S(1)}, f32[56,128]{1,0:T(8,128)S(1)}, f32[56,128]{1,0:T(8,128)S(1)}, f32[8,128]{1,0:T(8,128)S(1)}) custom-call(s32[5]{0:T(128)} %stack.31.flags.refs_0_, f32[2,8,3200]{2,1,0:T(8,128)} %bitcast.32, f32[1,1024]{1,0:T(1,128)} %bitcast.30, s32[1,1024]{1,0:T(1,128)} %bitcast.16, f32[1,1024]{1,0:T(1,128)} %bitcast.21, ...), custom_call_target="tpu_custom_call" | custom-call | tf_op jit(solution)/shard_map/begin/pallas_call | solution.py:340
  5.5 2.9 %collective-permute-start = (f32[56,128]{1,0:T(8,128)S(1)}, f32[56,128]{1,0:T(8,128)S(1)}, u32[]{:S(2)}, u32[]{:S(2)}) collective-permute-start(f32[56,128]{1,0:T(8,128)S(1)} %get-tuple-element.33), channel_id=1, source_target_pairs={{0,2},{2,0},{4,6},{6,4},{8,10},{10,8},{12,14},{14,12},{16,18},{18,... | collective-permute-start | bytes 86024 | tf_op jit(solution)/shard_map/ppermute | solution.py:362
  10.5 0.9 %prepare.1 = (s32[8,1024]{1,0:T(8,128)S(1)}, f32[3,8,1024]{2,1,0:T(8,128)S(1)}) custom-call(s32[5]{0:T(128)} %stack.31.flags.refs_0_, s32[6,1024]{1,0:T(8,128)} %neighbours.1, f32[2,6,1024]{2,1,0:T(8,128)} %copy.16.grad_weights, f32[6,1024]{1,0:T(8,128)} %lap_weights.1), custom_call_target="tpu_custom_call" | custom-call | tf_op jit(solution)/shard_map/prepare/pallas_call | solution.py:347
  12.1 4.9 %step.4 = (f32[48,1024]{1,0:T(8,128)S(1)}, f32[1,1024]{1,0:T(1,128)S(1)}, f32[56,128]{1,0:T(8,128)S(1)}, f32[56,128]{1,0:T(8,128)S(1)}, f32[8,128]{1,0:T(8,128)S(1)}) custom-call(s32[5]{0:T(128)} %stack.31.flags.refs_0_, f32[8,128]{1,0:T(8,128)S(1)} %get-tuple-element.31.refs_1_, f32[48,1024]{1,0:T(8,128)S(1)} %get-tuple-element.32.refs_2_, ...), custom_call_target="tpu_custom_call" | custom-call | tf_op jit(solution)/shard_map/step/pallas_call | solution.py:387
  17.0 4.3 %collective-permute-start.2 = (f32[56,128]{1,0:T(8,128)S(1)}, f32[56,128]{1,0:T(8,128)S(1)}, u32[]{:S(2)}, u32[]{:S(2)}) collective-permute-start(f32[56,128]{1,0:T(8,128)S(1)} %get-tuple-element.40), channel_id=1, source_target_pairs={{0,2},{2,0},{4,6},{6,4},{8,10},{10,8},{12,14},{14,12},{16,18},{18,... | collective-permute-start | bytes 86024 | tf_op jit(solution)/shard_map/ppermute | solution.py:362
  22.0 1.2 %collective-permute-done.2.refs_4_ = f32[56,128]{1,0:T(8,128)S(1)} collective-permute-done((f32[56,128]{1,0:T(8,128)S(1)}, f32[56,128]{1,0:T(8,128)S(1)}, u32[]{:S(2)}, u32[]{:S(2)}) %collective-permute-start.2) | collective-permute-done | bytes 28704 | tf_op jit(solution)/shard_map/ppermute | solution.py:362
  23.2 4.9 %step.5 = (f32[48,1024]{1,0:T(8,128)S(1)}, f32[1,1024]{1,0:T(1,128)S(1)}, f32[56,128]{1,0:T(8,128)S(1)}, f32[56,128]{1,0:T(8,128)S(1)}, f32[8,128]{1,0:T(8,128)S(1)}) custom-call(s32[5]{0:T(128)} %stack.31.flags.refs_0_, f32[8,128]{1,0:T(8,128)S(1)} %get-tuple-element.37.refs_1_, f32[48,1024]{1,0:T(8,128)S(1)} %get-tuple-element.38.refs_2_, ...), custom_call_target="tpu_custom_call" | custom-call | tf_op jit(solution)/shard_map/step/pallas_call | solution.py:387
  28.1 5.8 %collective-permute-start.4 = (f32[56,128]{1,0:T(8,128)S(1)}, f32[56,128]{1,0:T(8,128)S(1)}, u32[]{:S(2)}, u32[]{:S(2)}) collective-permute-start(f32[56,128]{1,0:T(8,128)S(1)} %get-tuple-element.45), channel_id=1, source_target_pairs={{0,2},{2,0},{4,6},{6,4},{8,10},{10,8},{12,14},{14,12},{16,18},{18,... | collective-permute-start | bytes 86024 | tf_op jit(solution)/shard_map/ppermute | solution.py:362
  34.6 1.2 %collective-permute-done.4.refs_4_ = f32[56,128]{1,0:T(8,128)S(1)} collective-permute-done((f32[56,128]{1,0:T(8,128)S(1)}, f32[56,128]{1,0:T(8,128)S(1)}, u32[]{:S(2)}, u32[]{:S(2)}) %collective-permute-start.4) | collective-permute-done | bytes 28704 | tf_op jit(solution)/shard_map/ppermute | solution.py:362
  35.8 5.0 %step.6 = (f32[48,1024]{1,0:T(8,128)S(1)}, f32[1,1024]{1,0:T(1,128)S(1)}, f32[56,128]{1,0:T(8,128)S(1)}, f32[56,128]{1,0:T(8,128)S(1)}, f32[8,128]{1,0:T(8,128)S(1)}) custom-call(s32[5]{0:T(128)} %stack.31.flags.refs_0_, f32[8,128]{1,0:T(8,128)S(1)} %get-tuple-element.42.refs_1_, f32[48,1024]{1,0:T(8,128)S(1)} %get-tuple-element.43.refs_2_, ...), custom_call_target="tpu_custom_call" | custom-call | tf_op jit(solution)/shard_map/step/pallas_call | solution.py:387
  40.8 6.4 %collective-permute-start.6 = (f32[56,128]{1,0:T(8,128)S(1)}, f32[56,128]{1,0:T(8,128)S(1)}, u32[]{:S(2)}, u32[]{:S(2)}) collective-permute-start(f32[56,128]{1,0:T(8,128)S(1)} %get-tuple-element.50), channel_id=1, source_target_pairs={{0,2},{2,0},{4,6},{6,4},{8,10},{10,8},{12,14},{14,12},{16,18},{18,... | collective-permute-start | bytes 86024 | tf_op jit(solution)/shard_map/ppermute | solution.py:362
  47.8 1.2 %collective-permute-done.6.refs_4_ = f32[56,128]{1,0:T(8,128)S(1)} collective-permute-done((f32[56,128]{1,0:T(8,128)S(1)}, f32[56,128]{1,0:T(8,128)S(1)}, u32[]{:S(2)}, u32[]{:S(2)}) %collective-permute-start.6) | collective-permute-done | bytes 28704 | tf_op jit(solution)/shard_map/ppermute | solution.py:362
  49.0 5.4 %step.7 = (f32[2,8,1024]{2,1,0:T(8,128)}, f32[8,1024]{1,0:T(8,128)}, f32[1,1024]{1,0:T(1,128)S(1)}, f32[8,128]{1,0:T(8,128)S(1)}) custom-call(s32[5]{0:T(128)} %stack.31.flags.refs_0_, f32[8,128]{1,0:T(8,128)S(1)} %get-tuple-element.47.refs_1_, f32[48,1024]{1,0:T(8,128)S(1)} %get-tuple-element.48.refs_2_, f32[1,1024]{1,0:T(1,128)S(1)} %get-tuple-element.49.refs_3_, ...), custom_call_target="tpu_custom_call" | custom-call | tf_op jit(solution)/shard_map/step/pallas_call | solution.py:387
  54.3 6.2 %collective-permute-start.8 = (f32[8,128]{1,0:T(8,128)S(1)}, f32[8,128]{1,0:T(8,128)S(1)}, u32[]{:S(2)}, u32[]{:S(2)}) collective-permute-start(f32[8,128]{1,0:T(8,128)S(1)} %get-tuple-element.54), channel_id=1, source_target_pairs={{0,2},{2,0},{4,6},{6,4},{8,10},{10,8},{12,14},{14,12},{16,18},{18,... | collective-permute-start | bytes 12296 | tf_op jit(solution)/shard_map/ppermute | solution.py:406
  60.6 1.6 %collective-permute-done.8 = f32[8,128]{1,0:T(8,128)S(1)} collective-permute-done((f32[8,128]{1,0:T(8,128)S(1)}, f32[8,128]{1,0:T(8,128)S(1)}, u32[]{:S(2)}, u32[]{:S(2)}) %collective-permute-start.8) | collective-permute-done | bytes 4128 | tf_op jit(solution)/shard_map/ppermute | solution.py:406
  62.1 3.5 %collective-permute-start.9 = (f32[8,128]{1,0:T(8,128)S(1)}, f32[8,128]{1,0:T(8,128)S(1)}, u32[]{:S(2)}, u32[]{:S(2)}) collective-permute-start(f32[8,128]{1,0:T(8,128)S(1)} %add.17), channel_id=1, source_target_pairs={{0,4},{2,6},{4,0},{6,2},{8,12},{10,14},{12,8},{14,10},{16,20},{18,... | collective-permute-start | bytes 12296 | tf_op jit(solution)/shard_map/ppermute | solution.py:406
  65.6 1.6 %collective-permute-done.9 = f32[8,128]{1,0:T(8,128)S(1)} collective-permute-done((f32[8,128]{1,0:T(8,128)S(1)}, f32[8,128]{1,0:T(8,128)S(1)}, u32[]{:S(2)}, u32[]{:S(2)}) %collective-permute-start.9) | collective-permute-done | bytes 4128 | tf_op jit(solution)/shard_map/ppermute | solution.py:406
  67.2 2.5 %collective-permute-start.10 = (f32[8,128]{1,0:T(8,128)S(1)}, f32[8,128]{1,0:T(8,128)S(1)}, u32[]{:S(2)}, u32[]{:S(2)}) collective-permute-start(f32[8,128]{1,0:T(8,128)S(1)} %add.18), channel_id=1, source_target_pairs={{0,8},{2,10},{4,12},{6,14},{8,0},{10,2},{12,4},{14,6},{16,24},{18,... | collective-permute-start | bytes 12296 | tf_op jit(solution)/shard_map/ppermute | solution.py:406
  69.7 1.6 %collective-permute-done.10 = f32[8,128]{1,0:T(8,128)S(1)} collective-permute-done((f32[8,128]{1,0:T(8,128)S(1)}, f32[8,128]{1,0:T(8,128)S(1)}, u32[]{:S(2)}, u32[]{:S(2)}) %collective-permute-start.10) | collective-permute-done | bytes 4128 | tf_op jit(solution)/shard_map/ppermute | solution.py:406
  71.3 3.0 %collective-permute-start.11 = (f32[8,128]{1,0:T(8,128)S(1)}, f32[8,128]{1,0:T(8,128)S(1)}, u32[]{:S(2)}, u32[]{:S(2)}) collective-permute-start(f32[8,128]{1,0:T(8,128)S(1)} %add.19), channel_id=1, source_target_pairs={{0,16},{2,18},{4,20},{6,22},{8,24},{10,26},{12,28},{14,30},{16,0},... | collective-permute-start | bytes 12296 | tf_op jit(solution)/shard_map/ppermute | solution.py:406
  74.3 1.6 %collective-permute-done.11 = f32[8,128]{1,0:T(8,128)S(1)} collective-permute-done((f32[8,128]{1,0:T(8,128)S(1)}, f32[8,128]{1,0:T(8,128)S(1)}, u32[]{:S(2)}, u32[]{:S(2)}) %collective-permute-start.11) | collective-permute-done | bytes 4128 | tf_op jit(solution)/shard_map/ppermute | solution.py:406
  76.6 1.3 %slice_reduce_fusion = f32[4]{0:T(128)} fusion(f32[8,128]{1,0:T(8,128)} %get-tuple-element.57), kind=kLoop, calls=%fused_computation.4 | loop fusion | bytes 32 | tf_op jit(solution)/shard_map/slice | solution.py:415
  (35 shorter events, 6.0 us)
Async XLA Ops:
  0.7 0.8 %copy-start.7 = (f32[8]{0:T(128)S(1)}, f32[8]{0:T(128)}, u32[]{:S(2)}) copy-start(f32[8]{0:T(128)} %param.18) | copy-start | bytes 100
  0.7 0.9 %copy-start.6 = (f32[8,1024]{1,0:T(8,128)S(1)}, f32[8,1024]{1,0:T(8,128)}, u32[]{:S(2)}) copy-start(f32[8,1024]{1,0:T(8,128)} %param.12) | copy-start | bytes 98308
  4.4 5.4 %copy-start.5 = (f32[2,6,1024]{2,0,1:T(2,128)S(1)}, f32[2,6,1024]{2,0,1:T(2,128)}, u32[]{:S(2)}) copy-start(f32[2,6,1024]{2,0,1:T(2,128)} %param.14) | copy-start | bytes 147460
  5.5 5.8 %collective-permute-start = (f32[56,128]{1,0:T(8,128)S(1)}, f32[56,128]{1,0:T(8,128)S(1)}, u32[]{:S(2)}, u32[]{:S(2)}) collective-permute-start(f32[56,128]{1,0:T(8,128)S(1)} %get-tuple-element.33), channel_id=1, source_target_pairs={{0,2},{2,0},{4,6},{6,4},{8,10},{10,8},{12,14},{14,12},{16,18},{18,... | collective-permute-start | bytes 86024 | tf_op jit(solution)/shard_map/ppermute | solution.py:362
  8.4 2.9 %collective-permute-start.1 = (f32[56,128]{1,0:T(8,128)S(1)}, f32[56,128]{1,0:T(8,128)S(1)}, u32[]{:S(2)}, u32[]{:S(2)}) collective-permute-start(f32[56,128]{1,0:T(8,128)S(1)} %get-tuple-element.34), channel_id=1, source_target_pairs={{0,0},{2,4},{4,2},{6,8},{8,6},{10,12},{12,10},{14,16},{16,14},{18,... | collective-permute-start | bytes 86024 | tf_op jit(solution)/shard_map/ppermute | solution.py:362
  10.5 1.0 %copy-start.2 = (f32[1024]{0:T(1024)S(1)}, f32[1024]{0:T(1024)}, u32[]{:S(2)}) copy-start(f32[1024]{0:T(1024)} %param.16) | copy-start | bytes 12292
  10.5 1.0 %copy-start.4 = (f32[1024]{0:T(1024)S(1)}, f32[1024]{0:T(1024)}, u32[]{:S(2)}) copy-start(f32[1024]{0:T(1024)} %param.13) | copy-start | bytes 12292
  11.4 0.7 copy-start.1
  11.4 0.7 copy-start
  11.4 0.7 copy-start.3
  17.0 6.1 %collective-permute-start.2 = (f32[56,128]{1,0:T(8,128)S(1)}, f32[56,128]{1,0:T(8,128)S(1)}, u32[]{:S(2)}, u32[]{:S(2)}) collective-permute-start(f32[56,128]{1,0:T(8,128)S(1)} %get-tuple-element.40), channel_id=1, source_target_pairs={{0,2},{2,0},{4,6},{6,4},{8,10},{10,8},{12,14},{14,12},{16,18},{18,... | collective-permute-start | bytes 86024 | tf_op jit(solution)/shard_map/ppermute | solution.py:362
  21.3 1.9 %collective-permute-start.3 = (f32[56,128]{1,0:T(8,128)S(1)}, f32[56,128]{1,0:T(8,128)S(1)}, u32[]{:S(2)}, u32[]{:S(2)}) collective-permute-start(f32[56,128]{1,0:T(8,128)S(1)} %get-tuple-element.41), channel_id=1, source_target_pairs={{0,0},{2,4},{4,2},{6,8},{8,6},{10,12},{12,10},{14,16},{16,14},{18,... | collective-permute-start | bytes 86024 | tf_op jit(solution)/shard_map/ppermute | solution.py:362
  28.1 7.7 %collective-permute-start.4 = (f32[56,128]{1,0:T(8,128)S(1)}, f32[56,128]{1,0:T(8,128)S(1)}, u32[]{:S(2)}, u32[]{:S(2)}) collective-permute-start(f32[56,128]{1,0:T(8,128)S(1)} %get-tuple-element.45), channel_id=1, source_target_pairs={{0,2},{2,0},{4,6},{6,4},{8,10},{10,8},{12,14},{14,12},{16,18},{18,... | collective-permute-start | bytes 86024 | tf_op jit(solution)/shard_map/ppermute | solution.py:362
  33.9 1.9 %collective-permute-start.5 = (f32[56,128]{1,0:T(8,128)S(1)}, f32[56,128]{1,0:T(8,128)S(1)}, u32[]{:S(2)}, u32[]{:S(2)}) collective-permute-start(f32[56,128]{1,0:T(8,128)S(1)} %get-tuple-element.46), channel_id=1, source_target_pairs={{0,0},{2,4},{4,2},{6,8},{8,6},{10,12},{12,10},{14,16},{16,14},{18,... | collective-permute-start | bytes 86024 | tf_op jit(solution)/shard_map/ppermute | solution.py:362
  40.8 8.2 %collective-permute-start.6 = (f32[56,128]{1,0:T(8,128)S(1)}, f32[56,128]{1,0:T(8,128)S(1)}, u32[]{:S(2)}, u32[]{:S(2)}) collective-permute-start(f32[56,128]{1,0:T(8,128)S(1)} %get-tuple-element.50), channel_id=1, source_target_pairs={{0,2},{2,0},{4,6},{6,4},{8,10},{10,8},{12,14},{14,12},{16,18},{18,... | collective-permute-start | bytes 86024 | tf_op jit(solution)/shard_map/ppermute | solution.py:362
  47.1 1.9 %collective-permute-start.7 = (f32[56,128]{1,0:T(8,128)S(1)}, f32[56,128]{1,0:T(8,128)S(1)}, u32[]{:S(2)}, u32[]{:S(2)}) collective-permute-start(f32[56,128]{1,0:T(8,128)S(1)} %get-tuple-element.51), channel_id=1, source_target_pairs={{0,0},{2,4},{4,2},{6,8},{8,6},{10,12},{12,10},{14,16},{16,14},{18,... | collective-permute-start | bytes 86024 | tf_op jit(solution)/shard_map/ppermute | solution.py:362
  54.3 7.8 %collective-permute-start.8 = (f32[8,128]{1,0:T(8,128)S(1)}, f32[8,128]{1,0:T(8,128)S(1)}, u32[]{:S(2)}, u32[]{:S(2)}) collective-permute-start(f32[8,128]{1,0:T(8,128)S(1)} %get-tuple-element.54), channel_id=1, source_target_pairs={{0,2},{2,0},{4,6},{6,4},{8,10},{10,8},{12,14},{14,12},{16,18},{18,... | collective-permute-start | bytes 12296 | tf_op jit(solution)/shard_map/ppermute | solution.py:406
  62.1 5.1 %collective-permute-start.9 = (f32[8,128]{1,0:T(8,128)S(1)}, f32[8,128]{1,0:T(8,128)S(1)}, u32[]{:S(2)}, u32[]{:S(2)}) collective-permute-start(f32[8,128]{1,0:T(8,128)S(1)} %add.17), channel_id=1, source_target_pairs={{0,4},{2,6},{4,0},{6,2},{8,12},{10,14},{12,8},{14,10},{16,20},{18,... | collective-permute-start | bytes 12296 | tf_op jit(solution)/shard_map/ppermute | solution.py:406
  67.2 4.1 %collective-permute-start.10 = (f32[8,128]{1,0:T(8,128)S(1)}, f32[8,128]{1,0:T(8,128)S(1)}, u32[]{:S(2)}, u32[]{:S(2)}) collective-permute-start(f32[8,128]{1,0:T(8,128)S(1)} %add.18), channel_id=1, source_target_pairs={{0,8},{2,10},{4,12},{6,14},{8,0},{10,2},{12,4},{14,6},{16,24},{18,... | collective-permute-start | bytes 12296 | tf_op jit(solution)/shard_map/ppermute | solution.py:406
  71.3 4.6 %collective-permute-start.11 = (f32[8,128]{1,0:T(8,128)S(1)}, f32[8,128]{1,0:T(8,128)S(1)}, u32[]{:S(2)}, u32[]{:S(2)}) collective-permute-start(f32[8,128]{1,0:T(8,128)S(1)} %add.19), channel_id=1, source_target_pairs={{0,16},{2,18},{4,20},{6,22},{8,24},{10,26},{12,28},{14,30},{16,0},... | collective-permute-start | bytes 12296 | tf_op jit(solution)/shard_map/ppermute | solution.py:406
